TPU v7x, 32 devices: a whole 2x2x4 slice. The times are simulated.
32 devices in a mesh: tp: 4 (over z), cp: 8 (over y, x, core).
Axes of the slice: x: 2, y: 2, z: 4, core: 2. Of those that a mesh axis runs over, the one named last changes fastest.
Arguments:
- x_in: bfloat16 [8192, 2560], P('cp')
- positions: int32 [8192], P('cp')
- attn_gain: bfloat16 [2, 2560], replicated
- mlp_gain: bfloat16 [2, 2560], replicated
- w_query: bfloat16 [2, 2560, 2560], P(None, None, 'tp')
- b_query: bfloat16 [2, 2560], P(None, 'tp')
- w_key: bfloat16 [2, 2560, 2560], P(None, None, 'tp')
- b_key: bfloat16 [2, 2560], P(None, 'tp')
- w_value: bfloat16 [2, 2560, 2560], P(None, None, 'tp')
- b_value: bfloat16 [2, 2560], P(None, 'tp')
- w_out: bfloat16 [2, 2560, 2560], P(None, 'tp')
- w_gate: bfloat16 [2, 2560, 6912], P(None, None, 'tp')
- w_up: bfloat16 [2, 2560, 6912], P(None, None, 'tp')
- w_down: bfloat16 [2, 6912, 2560], P(None, 'tp')
Outputs:
- output 1: bfloat16 [8192, 2560], P('cp')
- output 2: bfloat16 [8192, 20, 128], P('cp', 'tp')
- output 3: bfloat16 [8192, 20, 128], P('cp', 'tp')
- output 4: bfloat16 [8192, 20, 128], P('cp', 'tp')
- output 5: bfloat16 [8192, 20, 128], P('cp', 'tp')
All inputs are finite; a program needn't handle non-finite values.
Results may differ from a plain program's by a relative error of at most 0.02.
Values are sent between devices in bfloat16 or wider.
A program may use at most 1 GiB of HBM per device.

v0:
```python
import jax
import jax.numpy as jnp
from jax import lax
from jax.sharding import PartitionSpec as P

HEAD_DIM = 128
WINDOW = 4096
QUERY_BLOCK = 128


def rms_norm(hidden, gain):
    hidden_f = hidden.astype(jnp.float32)
    variance = jnp.mean(hidden_f * hidden_f, axis=-1, keepdims=True)
    return (hidden_f * lax.rsqrt(variance + 1e-6) * gain.astype(jnp.float32)).astype(jnp.bfloat16)


def rope_tables(positions):
    inv_freq = 1.0 / (1000000.0 ** (jnp.arange(0, HEAD_DIM, 2, dtype=jnp.float32) / HEAD_DIM))
    angles = positions.astype(jnp.float32)[:, None] * inv_freq[None, :]
    return jnp.cos(angles)[:, None, :], jnp.sin(angles)[:, None, :]


def apply_rope(proj_f, cos_tab, sin_tab):
    half_dim = proj_f.shape[-1] // 2
    first_half = proj_f[..., :half_dim]
    second_half = proj_f[..., half_dim:]
    return jnp.concatenate([first_half * cos_tab - second_half * sin_tab, second_half * cos_tab + first_half * sin_tab], axis=-1)


def project(normed, weight, bias_vec):
    return jnp.dot(normed, weight, preferred_element_type=jnp.float32) + bias_vec.astype(jnp.float32)


def solution(mesh):
    cp_size = mesh.shape['cp']
    score_scale = HEAD_DIM ** -0.5

    def local_attention(queries, key_all, value_all, q_start, window):
        block_dev, q_heads, head_dim = queries.shape
        kv_heads = key_all.shape[1]
        group_size = q_heads // kv_heads
        block_len = min(block_dev, QUERY_BLOCK)
        sub_count = block_dev // block_len
        q_split = queries.reshape(sub_count, block_len, kv_heads, group_size, head_dim)
        key_pos = jnp.arange(key_all.shape[0])

        def one_block(block_in):
            sub_idx, q_blk = block_in
            query_pos = q_start + sub_idx * block_len + jnp.arange(block_len)
            scores = jnp.einsum('qkgd,skd->qkgs', q_blk, key_all, preferred_element_type=jnp.float32) * score_scale
            allowed = (key_pos[None, :] <= query_pos[:, None]) & (key_pos[None, :] > query_pos[:, None] - window)
            scores = jnp.where(allowed[:, None, None, :], scores, -jnp.inf)
            probs_bf = jax.nn.softmax(scores, axis=-1).astype(jnp.bfloat16)
            return jnp.einsum('qkgs,skd->qkgd', probs_bf, value_all, preferred_element_type=jnp.float32).astype(jnp.bfloat16)

        attn_out = lax.map(one_block, (jnp.arange(sub_count), q_split))
        return attn_out.reshape(block_dev, q_heads * head_dim)

    def local_step(x_in, positions, attn_gain, mlp_gain, w_query, b_query, w_key, b_key, w_value, b_value, w_out, w_gate, w_up, w_down):
        block_dev = x_in.shape[0]
        q_start = lax.axis_index('cp') * block_dev
        cos_tab, sin_tab = rope_tables(positions)
        hidden = x_in
        caches = []
        for layer_idx, window in ((0, block_dev * cp_size), (1, WINDOW)):
            normed = rms_norm(hidden, attn_gain[layer_idx])
            queries = apply_rope(project(normed, w_query[layer_idx], b_query[layer_idx]).reshape(block_dev, -1, HEAD_DIM), cos_tab, sin_tab).astype(jnp.bfloat16)
            key_cache = apply_rope(project(normed, w_key[layer_idx], b_key[layer_idx]).reshape(block_dev, -1, HEAD_DIM), cos_tab, sin_tab).astype(jnp.bfloat16)
            value_cache = project(normed, w_value[layer_idx], b_value[layer_idx]).astype(jnp.bfloat16).reshape(block_dev, -1, HEAD_DIM)
            key_all = lax.all_gather(key_cache, 'cp', axis=0, tiled=True)
            value_all = lax.all_gather(value_cache, 'cp', axis=0, tiled=True)
            attn_out = local_attention(queries, key_all, value_all, q_start, window)
            attn_part = jnp.dot(attn_out, w_out[layer_idx], preferred_element_type=jnp.float32).astype(jnp.bfloat16)
            hidden = (hidden.astype(jnp.float32) + lax.psum(attn_part, 'tp').astype(jnp.float32)).astype(jnp.bfloat16)
            normed = rms_norm(hidden, mlp_gain[layer_idx])
            gate_proj = jnp.dot(normed, w_gate[layer_idx], preferred_element_type=jnp.float32)
            up_proj = jnp.dot(normed, w_up[layer_idx], preferred_element_type=jnp.float32)
            activated = (jax.nn.silu(gate_proj) * up_proj).astype(jnp.bfloat16)
            down_part = jnp.dot(activated, w_down[layer_idx], preferred_element_type=jnp.float32).astype(jnp.bfloat16)
            hidden = (hidden.astype(jnp.float32) + lax.psum(down_part, 'tp').astype(jnp.float32)).astype(jnp.bfloat16)
            caches.append(key_cache)
            caches.append(value_cache)
        return hidden, caches[0], caches[1], caches[2], caches[3]

    weight_col = P(None, None, 'tp')
    bias_col = P(None, 'tp')
    weight_row = P(None, 'tp', None)
    replicated = P(None, None)
    cache_spec = P('cp', 'tp', None)
    in_specs = (P('cp', None), P('cp'), replicated, replicated, weight_col, bias_col, weight_col, bias_col, weight_col, bias_col, weight_row, weight_col, weight_col, weight_row)
    out_specs = (P('cp', None), cache_spec, cache_spec, cache_spec, cache_spec)
    return jax.shard_map(local_step, mesh=mesh, in_specs=in_specs, out_specs=out_specs, check_vma=False)
```

profile of v0, /device:TPU:0, one launch (start us, length us, event | category | flops | bytes accessed | tf_op | source)
XLA Modules:
  0.0 1878.0 jit_solution(18119052892608768716)
XLA Ops:
  63.9 52.4 %all-gather.5.cloned.1.call-done = bf16[8192,5,128]{2,0,1:T(8,128)(2,1)} async-done(((bf16[1024,5,128]{2,0,1:T(8,128)(2,1)}), bf16[8192,5,128]{2,0,1:T(8,128)(2,1)}) %all-gather.5.cloned.1.call-update) | async-done | bytes 10485776 | tf_op jit(solution)/shard_map/all_gather | solution.py:70
  116.4 65.5 %all-gather.7.cloned.1.call-done = bf16[8192,5,128]{2,0,1:T(8,128)(2,1)} async-done(((bf16[1024,5,128]{2,0,1:T(8,128)(2,1)}), bf16[8192,5,128]{2,0,1:T(8,128)(2,1)}) %all-gather.7.cloned.1.call-update) | async-done | bytes 10485776 | tf_op jit(solution)/shard_map/all_gather | solution.py:71
  182.1 298.1 %while.28 = (s32[]{:T(128)}, bf16[8,128,5,1,128]{4,1,2,3,0:T(8,128)(2,1)S(1)}, s32[8]{0:T(128)S(1)}, s32[]{:T(128)}, bf16[8,128,5,1,128]{4,1,0,2,3:T(8,128)(2,1)...) while((s32[]{:T(128)}, ...), condition=%wide.region_4.5_spmd.clone.clone, body=%wide.region_1.4_spmd.clone.clone.sunk | while | flops 2750495744 | bytes 88426632 | solution.py:56
  206.2 13.3 fusion.190
  221.7 11.5 fusion.188
  243.4 13.3 fusion.190
  258.9 11.5 fusion.188
  280.7 13.3 fusion.190
  317.9 13.3 fusion.190
  355.1 13.3 fusion.190
  392.4 13.3 fusion.190
  429.6 13.3 fusion.190
  466.9 13.3 fusion.190
  490.9 186.7 %all-reduce.5.cloned.1.call-done = bf16[1024,2560]{1,0:T(8,128)(2,1)} async-done(((bf16[1024,2560]{1,0:T(8,128)(2,1)}), bf16[1024,2560]{1,0:T(8,128)(2,1)}) %all-reduce.5.cloned.1.call-update) | async-done | bytes 5242896 | tf_op jit(solution)/shard_map/psum | solution.py:74
  686.2 14.0 fusion.70
  700.2 45.7 %fusion.80 = bf16[1024,2560]{1,0:T(8,128)(2,1)} fusion(bf16[2,1728,2560]{2,1,0:T(8,128)(2,1)} %param.31, f32[1024,1728]{0,1:T(8,128)} %fusion.70, bf16[2,2560,1728]{1,2,0:T(8,128)(2,1)} %param.29, bf16[1024,2560]{1,0:T(8,128)(2,1)} %copy-done, f32[2560]{0:T(1024)S(1)} %get-tuple-element.298, f32[1024]{0:T(1024)S(1)} %add_rsqrt_fusion.2), kind=kOutput, calls=%fused_computation.96 | convolution fusion | flops 18143117312 | bytes 35272704 | tf_op jit(solution)/shard_map/dot_general | solution.py:79
  746.3 186.5 %all-reduce.7.cloned.1.call-done = bf16[1024,2560]{1,0:T(8,128)(2,1)} async-done(((bf16[1024,2560]{1,0:T(8,128)(2,1)}), bf16[1024,2560]{1,0:T(8,128)(2,1)}) %all-reduce.7.cloned.1.call-update) | async-done | bytes 5242896 | tf_op jit(solution)/shard_map/psum | solution.py:80
  992.2 49.4 %all-gather.9.cloned.1.call-done = bf16[8192,5,128]{2,0,1:T(8,128)(2,1)} async-done(((bf16[1024,5,128]{2,0,1:T(8,128)(2,1)}), bf16[8192,5,128]{2,0,1:T(8,128)(2,1)}) %all-gather.9.cloned.1.call-update) | async-done | bytes 10485776 | tf_op jit(solution)/shard_map/all_gather | solution.py:70
  1041.5 65.3 %all-gather.11.cloned.1.call-done = bf16[8192,5,128]{2,0,1:T(8,128)(2,1)} async-done(((bf16[1024,5,128]{2,0,1:T(8,128)(2,1)}), bf16[8192,5,128]{2,0,1:T(8,128)(2,1)}) %all-gather.11.cloned.1.call-update) | async-done | bytes 10485776 | tf_op jit(solution)/shard_map/all_gather | solution.py:71
  1107.2 299.1 %while.29 = (s32[]{:T(128)}, bf16[8,128,5,1,128]{4,1,2,3,0:T(8,128)(2,1)S(1)}, s32[8]{0:T(128)S(1)}, s32[]{:T(128)}, bf16[8,128,5,1,128]{4,1,0,2,3:T(8,128)(2,1)...) while((s32[]{:T(128)}, ...), condition=%wide.region_12.13_spmd.clone.clone, body=%wide.region_9.12_spmd.clone.clone.sunk | while | flops 2750495744 | bytes 88426632 | solution.py:56
  1131.4 13.3 fusion.197
  1168.8 13.3 fusion.197
  1206.1 13.3 fusion.197
  1243.5 13.3 fusion.197
  1280.8 13.3 fusion.197
  1318.2 13.3 fusion.197
  1355.6 13.3 fusion.197
  1392.9 13.3 fusion.197
  1415.8 187.9 %all-reduce.9.cloned.1.call-done = bf16[1024,2560]{1,0:T(8,128)(2,1)} async-done(((bf16[1024,2560]{1,0:T(8,128)(2,1)}), bf16[1024,2560]{1,0:T(8,128)(2,1)}) %all-reduce.9.cloned.1.call-update) | async-done | bytes 5242896 | tf_op jit(solution)/shard_map/psum | solution.py:74
  1614.5 15.6 fusion.64
  1630.1 45.8 %fusion.83 = bf16[1024,2560]{1,0:T(8,128)(2,1)} fusion(bf16[2,1728,2560]{2,1,0:T(8,128)(2,1)} %param.31, f32[1024,1728]{0,1:T(8,128)} %fusion.64, bf16[2,2560,1728]{1,2,0:T(8,128)(2,1)} %param.29, bf16[1024,2560]{1,0:T(8,128)(2,1)} %get-tuple-element.336, f32[2560]{0:T(1024)S(1)} %copy-done.13, f32[1024]{0:T(1024)S(1)} %add_rsqrt_fusion), kind=kOutput, calls=%fused_computation.97 | convolution fusion | flops 18143117312 | bytes 35272704 | tf_op jit(solution)/shard_map/dot_general | solution.py:79
  1675.9 187.0 %all-reduce.11.cloned.1.call-done = bf16[1024,2560]{1,0:T(8,128)(2,1)} async-done(((bf16[1024,2560]{1,0:T(8,128)(2,1)}), bf16[1024,2560]{1,0:T(8,128)(2,1)}) %all-reduce.11.cloned.1.call-update) | async-done | bytes 5242896 | tf_op jit(solution)/shard_map/psum | solution.py:80
  (188 shorter events, 513.3 us)
Async XLA Ops:
  7.2 5.2 copy-start.14
  7.2 109.2 %all-gather.5.cloned.1.call-start = ((), (), s32[]{:S(2)}) async-start(), calls=%async_computation | async-start | bytes 11796480 | tf_op jit(solution)/shard_map/all_gather | solution.py:70
  7.2 5.8 copy-start.2
  20.5 5.4 copy-start.15
  35.3 6.0 copy-start.17
  43.2 5.4 copy-start.8
  43.2 5.4 copy-start.10
  48.7 1.9 copy-start.16
  50.5 131.3 %all-gather.7.cloned.1.call-start = ((), (), s32[]{:S(2)}) async-start(), calls=%async_computation.1 | async-start | bytes 11796480 | tf_op jit(solution)/shard_map/all_gather | solution.py:71
  51.1 11.0 copy-start.3
  51.2 11.0 copy-start.4
  62.1 615.5 %all-reduce.5.cloned.1.call-start = ((), (), s32[]{:S(2)}) async-start(), calls=%async_computation.2 | async-start | bytes 10485760 | tf_op jit(solution)/shard_map/psum | solution.py:74
  489.6 0.7 copy-start.12
  489.6 443.3 %all-reduce.7.cloned.1.call-start = ((), (), s32[]{:S(2)}) async-start(), calls=%async_computation.3 | async-start | bytes 10485760 | tf_op jit(solution)/shard_map/psum | solution.py:80
  683.9 2.4 copy-start
  745.9 192.9 %copy-start.11 = (f32[2560]{0:T(1024)S(1)}, f32[2560]{0:T(1024)}, u32[]{:S(2)}) copy-start(f32[2560]{0:T(1024)} %get-tuple-element.300) | copy-start | bytes 30724
  745.9 295.7 %all-gather.9.cloned.1.call-start = ((), (), s32[]{:S(2)}) async-start(), calls=%async_computation.4 | async-start | bytes 11796480 | tf_op jit(solution)/shard_map/all_gather | solution.py:70
  932.8 6.0 copy-start.1
  938.8 5.0 copy-start.18
  943.8 7.5 copy-start.7
  953.1 5.1 copy-start.19
  966.3 6.0 copy-start.9
  977.6 1.9 copy-start.20
  979.4 127.4 %all-gather.11.cloned.1.call-start = ((), (), s32[]{:S(2)}) async-start(), calls=%async_computation.5 | async-start | bytes 11796480 | tf_op jit(solution)/shard_map/all_gather | solution.py:71
  979.5 10.8 copy-start.5
  979.5 10.8 copy-start.6
  990.2 613.4 %all-reduce.9.cloned.1.call-start = ((), (), s32[]{:S(2)}) async-start(), calls=%async_computation.6 | async-start | bytes 10485760 | tf_op jit(solution)/shard_map/psum | solution.py:74
  1415.7 198.8 %copy-start.13 = (f32[2560]{0:T(1024)S(1)}, f32[2560]{0:T(1024)}, u32[]{:S(2)}) copy-start(f32[2560]{0:T(1024)} %get-tuple-element.297) | copy-start | bytes 30724
  1415.7 447.2 %all-reduce.11.cloned.1.call-start = ((), (), s32[]{:S(2)}) async-start(), calls=%async_computation.7 | async-start | bytes 10485760 | tf_op jit(solution)/shard_map/psum | solution.py:80
Sparse Core Ops, SparseCore 0:
  50.6 65.7 all-gather.4
  118.8 62.9 all-gather.6
  489.7 187.7 all-reduce.4
  746.0 186.8 all-reduce.6
  979.5 61.9 all-gather.8
  1043.9 62.9 all-gather.10
  1415.8 187.8 all-reduce.8
  1676.0 186.8 all-reduce.10
where the time goes:
time: 1880 us
  waiting for transfers between devices  981 us (52%)
  matrix products  578 us (31%)
  other arithmetic  241 us (13%)
  local copies, waits for them, and re-layouts  50.7 us (3%)
    psum x2, waiting for transfers between devices, local_step(): lax.psum(attn_part, 'tp').astype(jnp.float32)  375 us
    psum x2, waiting for transfers between devices, local_step(): lax.psum(down_part, 'tp').astype(jnp.float32)  373 us
    dot_general x16, matrix products, one_block(): jnp.einsum('qkgs,skd->qkgd', probs_bf, value_all, preferred_element_type=...  213 us
    dot_general x16, matrix products, one_block(): jnp.einsum('qkgd,skd->qkgs', q_blk, key_all, preferred_element_type=jnp.f...  184 us
    reduce_sum x16, other arithmetic, one_block(): probs_bf = jax.nn.softmax(scores, axis=-1).astype(jnp.bfloat16)  164 us
    all_gather x2, waiting for transfers between devices, local_step(): value_all = lax.all_gather(value_cache, 'cp', axis=0, tiled=True)  131 us
    all_gather x2, waiting for transfers between devices, local_step(): key_all = lax.all_gather(key_cache, 'cp', axis=0, tiled=True)  102 us
    dot_general x2, matrix products, local_step(): jnp.dot(activated, w_down[layer_idx], preferred_element_type=jnp.float32)  91.4 us
  transfers between devices with their start and end apart: 8, of which 8 were waited for; matrix products, arithmetic and copies ran while one was open for 1% of the time, Pallas kernels for 0%

commit v1 on v0

v1 whole, which is shorter than its diff:
```python
import functools

import jax
import jax.numpy as jnp
from jax import lax
from jax.experimental import pallas as pl
from jax.experimental.pallas import tpu as pltpu
from jax.sharding import PartitionSpec as P

MESH = pl.DeviceIdType.MESH
BF16 = jnp.bfloat16
F32 = jnp.float32
HEAD_DIM = 128
HEADS = 5
BLOCK = 1024
WIDTH = 2560
FFN = 1728
QKV = 3 * HEADS * HEAD_DIM
WINDOW_BLOCKS = 4
CHUNK = 256
PIECE = 64
TILE_Q = 512
EXP_SCALE = HEAD_DIM ** -0.5 * 1.4426950408889634
VMEM_LIMIT = 62 * 2 ** 20


def hbm():
    return pl.BlockSpec(memory_space=pl.ANY)


def vmem():
    return pl.BlockSpec(memory_space=pltpu.VMEM)


def normalize(rows, gain):
    rows_f = rows.astype(F32)
    variance = jnp.mean(rows_f * rows_f, axis=-1, keepdims=True)
    return (rows_f * lax.rsqrt(variance + 1e-6) * gain).astype(BF16)


def qkv_kernel(layer, x_ref, gain_ref, wq_ref, wk_ref, wv_ref, bias_ref, cos_ref, sin_ref,
               q_ref, k_ref, vt_ref, kout_ref, vout_ref, w_buf, sems):
    half = HEADS * HEAD_DIM
    loads = []
    for i, w in enumerate((wq_ref, wk_ref, wv_ref)):
        copy = pltpu.make_async_copy(w.at[layer], w_buf.at[i], sems.at[i])
        copy.start()
        loads.append(copy)
    gain = gain_ref[layer:layer + 1, :].astype(F32)
    for copy in loads:
        copy.wait()

    def chunk(j, _):
        rows = pl.ds(pl.multiple_of(j * CHUNK, CHUNK), CHUNK)
        normed = normalize(x_ref[rows, :], gain)
        cos = cos_ref[rows, :]
        sin = sin_ref[rows, :]
        for i in range(3):
            proj = jnp.dot(normed, w_buf[i], preferred_element_type=F32) + bias_ref[i:i + 1, :].astype(F32)
            for h in range(HEADS):
                part = proj[:, h * HEAD_DIM:(h + 1) * HEAD_DIM]
                cols = slice(h * HEAD_DIM, (h + 1) * HEAD_DIM)
                if i < 2:
                    part = (part * cos + pltpu.roll(part, HEAD_DIM // 2, 1) * sin).astype(BF16)
                if i == 0:
                    q_ref[h, rows, :] = part
                elif i == 1:
                    k_ref[h, rows, :] = part
                    kout_ref[rows, cols] = part
                else:
                    vout_ref[rows, cols] = part.astype(BF16)
                    vt_ref[h, :, rows] = part.T.astype(BF16)
        return 0

    lax.fori_loop(0, BLOCK // CHUNK, chunk, 0)


def qkv_call(layer, x, gain, wq, wk, wv, bias, cos, sin):
    shape = jax.ShapeDtypeStruct
    return pl.pallas_call(
        functools.partial(qkv_kernel, layer),
        out_shape=(
            shape((HEADS, BLOCK, HEAD_DIM), BF16),
            shape((HEADS, BLOCK, HEAD_DIM), BF16),
            shape((HEADS, HEAD_DIM, BLOCK), BF16),
            shape((BLOCK, HEADS * HEAD_DIM), BF16),
            shape((BLOCK, HEADS * HEAD_DIM), BF16),
        ),
        in_specs=[vmem(), vmem(), hbm(), hbm(), hbm(), vmem(), vmem(), vmem()],
        out_specs=(vmem(),) * 5,
        scratch_shapes=[
            pltpu.VMEM((3, WIDTH, HEADS * HEAD_DIM), BF16),
            pltpu.SemaphoreType.DMA((3,)),
        ],
        compiler_params=pltpu.CompilerParams(vmem_limit_bytes=VMEM_LIMIT),
        cost_estimate=pl.CostEstimate(flops=2 * BLOCK * WIDTH * QKV, bytes_accessed=20_000_000, transcendentals=0),
        name=f"qkv{layer}",
    )(x, gain, wq, wk, wv, bias, cos, sin)


def dot_rows(a, b):
    return lax.dot_general(a, b, (((1,), (1,)), ((), ())), preferred_element_type=F32)


def attention_kernel(windowed, q_ref, k_ref, vt_ref, o_ref, k_buf, v_buf, o_buf, m_s, l_s, a_s, s0, s1,
                     load_sem, send_sem, recv_sem, o_send, o_recv, o_local):
    z = lax.axis_index("tp")
    cp = lax.axis_index("cp")
    x_dev = cp + 2 - 4 * ((cp // 2) % 2)
    y_dev = cp + 4 - 8 * (cp // 4)
    c_dev = cp + 1 - 2 * (cp % 2)
    d_blk = x_dev + 4 - 8 * (x_dev // 4)

    barrier = pltpu.get_barrier_semaphore()
    for other in (x_dev, y_dev, c_dev):
        pl.semaphore_signal(barrier, inc=1, device_id=(z, other), device_id_type=MESH)
    for step in range(1, 4):
        pl.semaphore_signal(barrier, inc=1, device_id=(lax.rem(z + step, 4), cp), device_id_type=MESH)

    def load(h, which):
        src, dst = ((k_ref, k_buf), (vt_ref, v_buf))[which]
        return pltpu.make_async_copy(src.at[h], dst.at[h, cp], load_sem.at[h, which])

    for h in range(HEADS):
        load(h, 0).start()
        load(h, 1).start()
    pl.semaphore_wait(barrier, 6)

    def hop(h, slot, which, src_block, dev):
        buf = (k_buf, v_buf)[which]
        if src_block is None:
            src = (k_ref, vt_ref)[which].at[h]
            dst = buf.at[h, cp]
        else:
            src = buf.at[h, src_block]
            dst = buf.at[h, src_block]
        return pltpu.make_async_remote_copy(
            src_ref=src, dst_ref=dst, send_sem=send_sem.at[h, slot], recv_sem=recv_sem.at[h, slot],
            device_id=(z, dev), device_id_type=MESH)

    def own(h, action):
        for which in range(2):
            for slot, dev in ((0, x_dev), (2, y_dev), (4, c_dev)):
                action(hop(h, slot + which, which, None, dev))

    def forward_x(h, action):
        action(hop(h, 6, 0, x_dev, y_dev))
        action(hop(h, 8, 0, x_dev, c_dev))
        action(hop(h, 9, 1, x_dev, c_dev))

    def forward_y(h, action):
        action(hop(h, 7, 1, y_dev, x_dev))
        action(hop(h, 10, 0, y_dev, c_dev))
        action(hop(h, 11, 1, y_dev, c_dev))

    def start(copy):
        copy.start()

    def wait_send(copy):
        copy.wait_send()

    def received(h, slot, which, block):
        hop(h, slot, which, block, c_dev).wait_recv()

    def event_neighbours(h):
        received(h, 0, 0, x_dev)
        received(h, 1, 1, x_dev)
        forward_x(h, start)
        received(h, 2, 0, y_dev)
        received(h, 3, 1, y_dev)
        forward_y(h, start)

    def event_diagonal(h):
        received(h, 6, 0, d_blk)
        hop(h, 12, 0, d_blk, c_dev).start()
        received(h, 7, 1, d_blk)
        hop(h, 13, 1, d_blk, c_dev).start()

    def event_core(h):
        load(h, 0).wait()
        load(h, 1).wait()
        for slot in (4, 8, 10, 12):
            received(h, slot, 0, c_dev)
        for slot in (5, 9, 11, 13):
            received(h, slot, 1, c_dev)

    def o_cols(src_z, h):
        return o_ref.at[:, pl.ds(pl.multiple_of((src_z * HEADS + h) * HEAD_DIM, HEAD_DIM), HEAD_DIM)]

    def o_copy(h, target):
        return pltpu.make_async_remote_copy(
            src_ref=o_buf.at[h], dst_ref=o_cols(z, h), send_sem=o_send.at[h, target], recv_sem=o_recv.at[h, z],
            device_id=(target, cp), device_id_type=MESH)

    def o_forward(h):
        far = jnp.where(z == 1, 3, 0)
        target = jnp.where(z == 1, 0, 3)
        return pltpu.make_async_remote_copy(
            src_ref=o_cols(far, h), dst_ref=o_cols(far, h), send_sem=o_send.at[h, 4], recv_sem=o_recv.at[h, far],
            device_id=(target, cp), device_id_type=MESH)

    def o_received(h, src_z):
        pltpu.make_async_remote_copy(
            src_ref=o_buf.at[h], dst_ref=o_cols(src_z, h), send_sem=o_send.at[h, src_z], recv_sem=o_recv.at[h, src_z],
            device_id=(z, cp), device_id_type=MESH).wait_recv()

    sends_to = ((1, 2), (0, 2, 3), (3, 1, 0), (2, 1))

    def o_start(h):
        pltpu.make_async_copy(o_buf.at[h], o_cols(z, h), o_local.at[h]).start()
        for src in range(4):
            @pl.when(z == src)
            def _():
                for target in sends_to[src]:
                    o_copy(h, target).start()

    def o_pass(h):
        @pl.when((z == 1) | (z == 2))
        def _():
            o_received(h, jnp.where(z == 1, 3, 0))
            o_forward(h).start()

    key_iota = lax.broadcasted_iota(jnp.int32, (BLOCK, TILE_Q), 0)
    row_iota = lax.broadcasted_iota(jnp.int32, (BLOCK, TILE_Q), 1)

    def attend(h, t):
        q = q_ref[h, t * TILE_Q:(t + 1) * TILE_Q, :]

        def scores(j):
            return dot_rows(k_buf[h, j], q)

        def soft(s, j):
            m_old = m_s[...]
            m_new = jnp.maximum(m_old, jnp.max(s, axis=0, keepdims=True))
            alpha = jnp.exp2((m_old - m_new) * EXP_SCALE)
            p = jnp.exp2((s - m_new) * EXP_SCALE)
            l_s[...] = l_s[...] * alpha + jnp.sum(p, axis=0, keepdims=True)
            a_s[...] = a_s[...] * alpha + jnp.dot(v_buf[h, j], p.astype(BF16), preferred_element_type=F32)
            m_s[...] = m_new

        lo = jnp.maximum(cp - (WINDOW_BLOCKS - 1), 0) if windowed else 0
        count = cp - lo
        s0[...] = scores(cp)
        s1[...] = scores(jnp.minimum(lo, cp))
        s = jnp.where(key_iota <= row_iota + t * TILE_Q, s0[...], -1e30)
        m_new = jnp.max(s, axis=0, keepdims=True)
        p = jnp.exp2((s - m_new) * EXP_SCALE)
        l_s[...] = jnp.sum(p, axis=0, keepdims=True)
        a_s[...] = jnp.dot(v_buf[h, cp], p.astype(BF16), preferred_element_type=F32)
        m_s[...] = m_new

        def pair(i, _):
            j = lo + 2 * i
            s0[...] = scores(j + 1)
            soft(s1[...], j)
            s1[...] = scores(jnp.minimum(j + 2, cp))
            soft(s0[...], j + 1)
            return 0

        lax.fori_loop(0, count // 2, pair, 0)

        @pl.when(count % 2 == 1)
        def _():
            soft(s1[...], cp - 1)

        if windowed:
            @pl.when(cp >= WINDOW_BLOCKS)
            def _():
                s = scores(cp - WINDOW_BLOCKS)
                soft(jnp.where(key_iota > row_iota + t * TILE_Q, s, -1e30), cp - WINDOW_BLOCKS)

        o_buf[h, t * TILE_Q:(t + 1) * TILE_Q, :] = (a_s[...] / l_s[...]).T.astype(BF16)

    own(0, start)
    event_neighbours(0)
    own(1, start)
    own(2, start)
    event_diagonal(0)

    def head(h, _):
        event_core(h)
        attend(h, 0)

        @pl.when(h + 1 < HEADS)
        def _():
            event_neighbours(h + 1)

        @pl.when(h + 3 < HEADS)
        def _():
            own(h + 3, start)

        attend(h, 1)
        o_start(h)

        @pl.when(h + 1 < HEADS)
        def _():
            event_diagonal(h + 1)

        @pl.when(h >= 1)
        def _():
            o_pass(h - 1)
        return 0

    lax.fori_loop(0, HEADS, head, 0)
    o_pass(HEADS - 1)

    def drain(h, _):
        own(h, wait_send)
        forward_x(h, wait_send)
        forward_y(h, wait_send)
        hop(h, 12, 0, d_blk, c_dev).wait_send()
        hop(h, 13, 1, d_blk, c_dev).wait_send()
        pltpu.make_async_copy(o_buf.at[h], o_cols(z, h), o_local.at[h]).wait()
        for me in range(4):
            @pl.when(z == me)
            def _():
                for target in sends_to[me]:
                    o_copy(h, target).wait_send()
                for src in range(4):
                    if src != me and (me, src) not in ((1, 3), (2, 0)):
                        o_received(h, src)

        @pl.when((z == 1) | (z == 2))
        def _():
            o_forward(h).wait_send()
        return 0

    lax.fori_loop(0, HEADS, drain, 0)


def attention_call(layer, windowed, q, k, vt):
    return pl.pallas_call(
        functools.partial(attention_kernel, windowed),
        out_shape=jax.ShapeDtypeStruct((BLOCK, 4 * HEADS * HEAD_DIM), BF16),
        in_specs=[vmem(), hbm(), hbm()],
        out_specs=hbm(),
        scratch_shapes=[
            pltpu.VMEM((HEADS, 8, BLOCK, HEAD_DIM), BF16),
            pltpu.VMEM((HEADS, 8, HEAD_DIM, BLOCK), BF16),
            pltpu.VMEM((HEADS, BLOCK, HEAD_DIM), BF16),
            pltpu.VMEM((1, TILE_Q), F32),
            pltpu.VMEM((1, TILE_Q), F32),
            pltpu.VMEM((HEAD_DIM, TILE_Q), F32),
            pltpu.VMEM((BLOCK, TILE_Q), F32),
            pltpu.VMEM((BLOCK, TILE_Q), F32),
            pltpu.SemaphoreType.DMA((HEADS, 2)),
            pltpu.SemaphoreType.DMA((HEADS, 14)),
            pltpu.SemaphoreType.DMA((HEADS, 14)),
            pltpu.SemaphoreType.DMA((HEADS, 5)),
            pltpu.SemaphoreType.DMA((HEADS, 4)),
            pltpu.SemaphoreType.DMA((HEADS,)),
        ],
        compiler_params=pltpu.CompilerParams(
            vmem_limit_bytes=VMEM_LIMIT, collective_id=1 + layer, has_side_effects=True),
        cost_estimate=pl.CostEstimate(flops=50_000_000_000, bytes_accessed=40_000_000, transcendentals=0),
        name=f"attention{layer}",
    )(q, k, vt)


def mlp_kernel(layer, x_ref, gain_ref, wg_ref, wu_ref, wd_ref, out_ref,
               wg, wu, wd, xv, pv, rv, sv, load_sem, r_send, r_recv, s_send, s_recv, x_send, x_recv, x_local):
    z = lax.axis_index("tp")
    cp = lax.axis_index("cp")
    inner = (z == 1) | (z == 2)
    partner = z + 1 - 2 * (z % 2)
    middle = jnp.where(inner, 3 - z, z)
    per_chunk = CHUNK // PIECE
    pieces = BLOCK // PIECE

    loads = [
        pltpu.make_async_copy(x_ref, xv, load_sem.at[0]),
        pltpu.make_async_copy(wg_ref.at[layer], wg, load_sem.at[1]),
        pltpu.make_async_copy(wu_ref.at[layer], wu, load_sem.at[2]),
        pltpu.make_async_copy(wd_ref.at[layer], wd, load_sem.at[3]),
    ]
    for copy in loads:
        copy.start()

    barrier = pltpu.get_barrier_semaphore()
    pl.semaphore_signal(barrier, inc=1, device_id=(partner, cp), device_id_type=MESH)

    @pl.when(inner)
    def _():
        pl.semaphore_signal(barrier, inc=1, device_id=(3 - z, cp), device_id_type=MESH)
        pl.semaphore_wait(barrier, 2)

    @pl.when(jnp.logical_not(inner))
    def _():
        pl.semaphore_wait(barrier, 1)

    gain = gain_ref[layer:layer + 1, :].astype(F32)
    for copy in loads:
        copy.wait()

    def rows_of(i, size):
        return pl.ds(pl.multiple_of(i * size, size), size)

    def remote(src, dst, send, recv, i, dev):
        return pltpu.make_async_remote_copy(
            src_ref=src.at[rows_of(i, PIECE), :], dst_ref=dst.at[rows_of(i, PIECE), :],
            send_sem=send.at[i], recv_sem=recv.at[i], device_id=(dev, cp), device_id_type=MESH)

    def copy_r(i):
        return remote(pv, rv, r_send, r_recv, i, partner)

    def copy_s(i):
        return remote(pv, sv, s_send, s_recv, i, middle)

    def copy_x(i):
        return remote(xv, out_ref, x_send, x_recv, i, partner)

    def copy_local(i):
        return pltpu.make_async_copy(xv.at[rows_of(i, PIECE), :], out_ref.at[rows_of(i, PIECE), :], x_local.at[i])

    def compute(j):
        rows = rows_of(j, CHUNK)
        normed = normalize(xv[rows, :], gain)
        gate = jnp.dot(normed, wg[...], preferred_element_type=F32)
        up = jnp.dot(normed, wu[...], preferred_element_type=F32)
        act = (gate * jax.nn.sigmoid(gate) * up).astype(BF16)
        pv[rows, :] = jnp.dot(act, wd[...], preferred_element_type=F32).astype(BF16)

    def add_end(i):
        rows = rows_of(i, PIECE)
        copy_r(i).wait_recv()
        pv[rows, :] = (pv[rows, :].astype(F32) + rv[rows, :].astype(F32)).astype(BF16)
        copy_s(i).start()

    def add_middle(i):
        rows = rows_of(i, PIECE)
        copy_s(i).wait_recv()
        total = pv[rows, :].astype(F32) + sv[rows, :].astype(F32)
        xv[rows, :] = (xv[rows, :].astype(F32) + total).astype(BF16)
        copy_x(i).start()
        copy_local(i).start()

    def step(j, _):
        @pl.when(j < BLOCK // CHUNK)
        def _():
            compute(j)

            @pl.when(jnp.logical_not(inner))
            def _():
                for k in range(per_chunk):
                    copy_r(j * per_chunk + k).start()

        @pl.when(inner & (j >= 1))
        def _():
            def piece(k, _):
                i = (j - 1) * per_chunk + k
                add_end(i)

                @pl.when(i >= 1)
                def _():
                    add_middle(i - 1)
                return 0

            lax.fori_loop(0, per_chunk, piece, 0)
        return 0

    lax.fori_loop(0, BLOCK // CHUNK + 1, step, 0)

    @pl.when(inner)
    def _():
        add_middle(pieces - 1)

        def drain(i, _):
            copy_s(i).wait_send()
            copy_x(i).wait_send()
            copy_local(i).wait()
            return 0

        lax.fori_loop(0, pieces, drain, 0)

    @pl.when(jnp.logical_not(inner))
    def _():
        def drain(i, _):
            copy_r(i).wait_send()
            copy_x(i).wait_recv()
            return 0

        lax.fori_loop(0, pieces, drain, 0)


def mlp_call(layer, x, gain, wg, wu, wd):
    pieces = BLOCK // PIECE
    return pl.pallas_call(
        functools.partial(mlp_kernel, layer),
        out_shape=jax.ShapeDtypeStruct((BLOCK, WIDTH), BF16),
        in_specs=[hbm(), vmem(), hbm(), hbm(), hbm()],
        out_specs=hbm(),
        scratch_shapes=[
            pltpu.VMEM((WIDTH, FFN), BF16),
            pltpu.VMEM((WIDTH, FFN), BF16),
            pltpu.VMEM((FFN, WIDTH), BF16),
            pltpu.VMEM((BLOCK, WIDTH), BF16),
            pltpu.VMEM((BLOCK, WIDTH), BF16),
            pltpu.VMEM((BLOCK, WIDTH), BF16),
            pltpu.VMEM((BLOCK, WIDTH), BF16),
            pltpu.SemaphoreType.DMA((4,)),
        ] + [pltpu.SemaphoreType.DMA((pieces,))] * 7,
        compiler_params=pltpu.CompilerParams(
            vmem_limit_bytes=VMEM_LIMIT, collective_id=3 + layer, has_side_effects=True),
        cost_estimate=pl.CostEstimate(flops=100_000_000_000, bytes_accessed=40_000_000, transcendentals=0),
        name=f"mlp{layer}",
    )(x, gain, wg, wu, wd)


def solution(mesh):
    def local_step(x_in, positions, attn_gain, mlp_gain, w_query, b_query, w_key, b_key, w_value, b_value,
                   w_out, w_gate, w_up, w_down):
        cp = lax.axis_index("cp")
        rows = w_out.shape[1] // 8
        w_slice = lax.dynamic_slice_in_dim(w_out, cp * rows, rows, axis=1)
        w_full = [lax.all_gather(w_slice[l], ("tp", "cp"), axis=0, tiled=True) for l in range(2)]

        inv_freq = 1.0 / (1000000.0 ** (jnp.arange(0, HEAD_DIM, 2, dtype=F32) / HEAD_DIM))
        angles = positions.astype(F32)[:, None] * inv_freq[None, :]
        cos, sin = jnp.cos(angles), jnp.sin(angles)
        cos = jnp.concatenate([cos, cos], axis=1)
        sin = jnp.concatenate([-sin, sin], axis=1)

        hidden = x_in
        caches = []
        for layer in range(2):
            bias = jnp.stack([b_query[layer], b_key[layer], b_value[layer]])
            q, k, vt, k_out, v_out = qkv_call(layer, hidden, attn_gain, w_query, w_key, w_value, bias, cos, sin)
            heads = attention_call(layer, layer == 1, q, k, vt)
            hidden = (hidden.astype(F32) + jnp.dot(heads, w_full[layer], preferred_element_type=F32)).astype(BF16)
            hidden = mlp_call(layer, hidden, mlp_gain, w_gate, w_up, w_down)
            caches.append(k_out.reshape(BLOCK, HEADS, HEAD_DIM))
            caches.append(v_out.reshape(BLOCK, HEADS, HEAD_DIM))
        return hidden, caches[0], caches[1], caches[2], caches[3]

    weight_col = P(None, None, "tp")
    bias_col = P(None, "tp")
    weight_row = P(None, "tp", None)
    replicated = P(None, None)
    cache_spec = P("cp", "tp", None)
    in_specs = (P("cp", None), P("cp"), replicated, replicated, weight_col, bias_col, weight_col, bias_col,
                weight_col, bias_col, weight_row, weight_col, weight_col, weight_row)
    out_specs = (P("cp", None), cache_spec, cache_spec, cache_spec, cache_spec)
    return jax.shard_map(local_step, mesh=mesh, in_specs=in_specs, out_specs=out_specs, check_vma=False)
```

time: 1880 us -> 816 us (0.43)
  waiting for transfers between devices: 981 us -> 0.75 us
  Pallas kernels: 0 us -> 682 us
  matrix products: 578 us -> 41.2 us
  other arithmetic: 241 us -> 5.17 us
    psum x4 -> x0, waiting for transfers between devices: 748 us -> none  [the longest x2 375 us: local_step(): lax.psum(attn_part, 'tp').astype(jnp.float32)]
    pallas_call x0 -> x6, Pallas kernels: none -> 682 us  [the longest x2 332 us: attention_call(): pl.pallas_call(functools.partial(attention_kernel, windowed), out_shape=j...]
    dot_general x44 -> x2, matrix products: 578 us -> 41.2 us  [local_step(): jnp.dot(heads, w_full[layer], preferred_element_type=F32)]
    all_gather x4 -> x2, waiting for transfers between devices: 233 us -> 0.04 us  [local_step(): lax.all_gather(w_slice[l], ('tp', 'cp'), axis=0, tiled=True)]
    reduce_sum x20 -> x0, other arithmetic: 190 us -> none  [the longest x16 164 us: one_block(): probs_bf = jax.nn.softmax(scores, axis=-1).astype(jnp.bfloat16)]
    unnamed x50 -> x17, local copies, waits for them, and re-layouts: 25.5 us -> 57.4 us
  transfers between devices with their start and end apart: 8 -> 2, of which waited for: 8 -> 0; matrix products, arithmetic and copies ran while one was open for 1% -> 10% of each run, Pallas kernels for 0% -> 65%
where the time goes in v1:
time: 816 us; the launch traced here: 808 us
  Pallas kernels  682 us (84%)
  local copies, waits for them, and re-layouts  64.2 us (8%)
  matrix products  41.2 us (5%)
  between operations  14.6 us (2%)
    pallas_call x2, Pallas kernels, attention_call(): pl.pallas_call(functools.partial(attention_kernel, windowed), out_shape=j...  332 us
    pallas_call x2, Pallas kernels, mlp_call(): pl.pallas_call(functools.partial(mlp_kernel, layer), out_shape=jax.ShapeD...  305 us
    unnamed x17, local copies, waits for them, and re-layouts  57.4 us
    pallas_call x2, Pallas kernels, qkv_call(): pl.pallas_call(functools.partial(qkv_kernel, layer), out_shape=(shape((HE...  45.4 us
    dot_general x2, matrix products, local_step(): jnp.dot(heads, w_full[layer], preferred_element_type=F32)  41.2 us
  transfers between devices with their start and end apart: 2, of which 0 were waited for; matrix products, arithmetic and copies ran while one was open for 10% of the time, Pallas kernels for 65%

profile of v1, /device:TPU:0, one launch (start us, length us, event | category | flops | bytes accessed | tf_op | source)
XLA Modules:
  0.0 808.2 jit_solution(262461182471717261)
XLA Ops:
  7.2 0.0 all-gather.5.cloned.1.call-start
  7.2 2.1 constant_dynamic-slice_fusion.1
  9.3 0.0 all-gather.5.cloned.1.call-update
  9.4 0.0 all-gather.7.cloned.1.call-start
  9.4 0.7 all-gather.7.cloned.1.call-update
  10.1 0.7 convert_element_type.16
  10.8 23.2 %copy.27.wg_ref = bf16[2,2560,1728]{2,1,0:T(8,128)(2,1)} copy(bf16[2,2560,1728]{1,2,0:T(8,128)(2,1)} %param.25) | data formatting | bytes 35389440 | tf_op args[11]
  34.0 23.2 %copy.28.wu_ref = bf16[2,2560,1728]{2,1,0:T(8,128)(2,1)} copy(bf16[2,2560,1728]{1,2,0:T(8,128)(2,1)} %param.26) | data formatting | bytes 35389440 | tf_op args[12]
  57.3 0.6 pad_maximum_fusion.2.bias_ref
  57.9 1.9 fusion.8
  59.8 1.4 pad_maximum_fusion
  61.2 22.6 %qkv0.1 = (bf16[5,1024,128]{2,1,0:T(8,128)(2,1)}, bf16[5,1024,128]{2,1,0:T(8,128)(2,1)}, bf16[5,128,1024]{2,1,0:T(8,128)(2,1)}, bf16[1024,640]{1,0:T(8,128)(2,1)}, bf16[1024,640]{1,0:T(8,128)(2,1)}) custom-call(bf16[1024,2560]{1,0:T(8,128)(2,1)} %x_ref.1, bf16[2,2560]{1,0:T(2,128)(2,1)} %gain_ref.6, bf16[2,2560,640]{2,1,0:T(8,128)(2,1)} %wq_ref.3, ...), custom_call_target="tpu_custom_call" | custom-call | flops 10066329600 | bytes 20000000 | tf_op jit(solution)/shard_map/qkv0/pallas_call | solution.py:80
  83.8 1.7 copy.31
  85.5 1.4 copy.35
  86.9 0.6 copy.32
  87.6 1.4 copy.36
  89.0 0.6 pad_maximum_fusion.3.bias_ref
  89.6 194.6 %attention0.1 = bf16[1024,2560]{1,0:T(8,128)(2,1)} custom-call(bf16[5,1024,128]{2,1,0:T(8,128)(2,1)} %get-tuple-element.15.q_ref, bf16[5,1024,128]{2,1,0:T(8,128)(2,1)} %get-tuple-element.16.k_ref, bf16[5,128,1024]{2,1,0:T(8,128)(2,1)} %get-tuple-element.17.vt_ref), custom_call_target="tpu_custom_call" | custom-call | flops 49999998976 | bytes 40000000 | tf_op jit(solution)/shard_map/attention0/pallas_call | solution.py:332
  284.2 0.0 all-gather.5.cloned.1.call-done
  284.2 20.5 %add_convert_fusion.1.x_ref = bf16[1024,2560]{1,0:T(8,128)(2,1)} fusion(bf16[1024,2560]{1,0:T(8,128)(2,1)} %x_ref.1, bf16[1024,2560]{1,0:T(8,128)(2,1)} %attention0.1, bf16[1,2560,2560]{2,1,0:T(8,128)(2,1)} %all-gather.5.cloned.1.call-done), kind=kOutput, calls=%fused_computation.5 | convolution fusion | flops 13429637120 | bytes 28835840 | tf_op jit(solution)/shard_map/dot_general | solution.py:529
  304.7 151.1 %mlp0.1.x_ref = bf16[1024,2560]{1,0:T(8,128)(2,1)} custom-call(bf16[1024,2560]{1,0:T(8,128)(2,1)} %add_convert_fusion.1.x_ref, bf16[2,2560]{1,0:T(2,128)(2,1)} %gain_ref.7, bf16[2,2560,1728]{2,1,0:T(8,128)(2,1)} %copy.27.wg_ref, bf16[2,2560,1728]{2,1,0:T(8,128)(2,1)} %copy.28.wu_ref, bf16[2,1728,2560]{2,1,0:T(8,128)(2,1)} %wd_ref.3), custom_call_target="tpu_custom_call" | custom-call | flops 99999997952 | bytes 40000000 | tf_op jit(solution)/shard_map/mlp0/pallas_call | solution.py:487
  455.8 22.8 %qkv1.1 = (bf16[5,1024,128]{2,1,0:T(8,128)(2,1)}, bf16[5,1024,128]{2,1,0:T(8,128)(2,1)}, bf16[5,128,1024]{2,1,0:T(8,128)(2,1)}, bf16[1024,640]{1,0:T(8,128)(2,1)}, bf16[1024,640]{1,0:T(8,128)(2,1)}) custom-call(bf16[1024,2560]{1,0:T(8,128)(2,1)} %mlp0.1.x_ref, bf16[2,2560]{1,0:T(2,128)(2,1)} %gain_ref.6, bf16[2,2560,640]{2,1,0:T(8,128)(2,1)} %wq_ref.3, ...), custom_call_target="tpu_custom_call" | custom-call | flops 10066329600 | bytes 20000000 | tf_op jit(solution)/shard_map/qkv1/pallas_call | solution.py:80
  478.7 137.6 %attention1.1 = bf16[1024,2560]{1,0:T(8,128)(2,1)} custom-call(bf16[5,1024,128]{2,1,0:T(8,128)(2,1)} %get-tuple-element.18.q_ref, bf16[5,1024,128]{2,1,0:T(8,128)(2,1)} %get-tuple-element.19.k_ref, bf16[5,128,1024]{2,1,0:T(8,128)(2,1)} %get-tuple-element.20.vt_ref), custom_call_target="tpu_custom_call" | custom-call | flops 49999998976 | bytes 40000000 | tf_op jit(solution)/shard_map/attention1/pallas_call | solution.py:332
  616.2 0.0 all-gather.7.cloned.1.call-done
  616.3 20.7 %add_convert_fusion.x_ref = bf16[1024,2560]{1,0:T(8,128)(2,1)} fusion(bf16[1024,2560]{1,0:T(8,128)(2,1)} %mlp0.1.x_ref, bf16[1024,2560]{1,0:T(8,128)(2,1)} %attention1.1, bf16[1,2560,2560]{2,1,0:T(8,128)(2,1)} %all-gather.7.cloned.1.call-done), kind=kOutput, calls=%fused_computation.4 | convolution fusion | flops 13429637120 | bytes 28835840 | tf_op jit(solution)/shard_map/dot_general | solution.py:529
  637.0 153.5 %mlp1.1 = bf16[1024,2560]{1,0:T(8,128)(2,1)} custom-call(bf16[1024,2560]{1,0:T(8,128)(2,1)} %add_convert_fusion.x_ref, bf16[2,2560]{1,0:T(2,128)(2,1)} %gain_ref.7, bf16[2,2560,1728]{2,1,0:T(8,128)(2,1)} %copy.27.wg_ref, bf16[2,2560,1728]{2,1,0:T(8,128)(2,1)} %copy.28.wu_ref, bf16[2,1728,2560]{2,1,0:T(8,128)(2,1)} %wd_ref.3), custom_call_target="tpu_custom_call" | custom-call | flops 99999997952 | bytes 40000000 | tf_op jit(solution)/shard_map/mlp1/pallas_call | solution.py:487
  790.5 1.7 copy.33
  792.2 1.4 copy.37
  793.6 0.0 copy-done
  793.6 0.6 copy.34
  794.3 1.4 copy.38
  795.7 5.2 copy.40
  (12 shorter events, 0.0 us)
Async XLA Ops:
  7.2 277.0 %all-gather.5.cloned.1.call-start = ((), (), s32[]{:S(2)}) async-start(), calls=%async_computation | async-start | bytes 13516800 | tf_op jit(solution)/shard_map/all_gather | solution.py:515
  9.4 606.9 %all-gather.7.cloned.1.call-start = ((), (), s32[]{:S(2)}) async-start(), calls=%async_computation.1 | async-start | bytes 13516800 | tf_op jit(solution)/shard_map/all_gather | solution.py:515
  34.0 23.3 %copy-start.4 = (bf16[2,640]{1,0:T(2,128)(2,1)S(1)}, bf16[2,640]{1,0:T(2,128)(2,1)}, u32[]{:S(2)}) copy-start(bf16[2,640]{1,0:T(2,128)(2,1)} %param.23) | copy-start | bytes 7684
  34.0 23.3 %copy-start.2 = (bf16[2,640]{1,0:T(2,128)(2,1)S(1)}, bf16[2,640]{1,0:T(2,128)(2,1)}, u32[]{:S(2)}) copy-start(bf16[2,640]{1,0:T(2,128)(2,1)} %param.19) | copy-start | bytes 7684
  34.0 23.3 %copy-start.3 = (bf16[2,640]{1,0:T(2,128)(2,1)S(1)}, bf16[2,640]{1,0:T(2,128)(2,1)}, u32[]{:S(2)}) copy-start(bf16[2,640]{1,0:T(2,128)(2,1)} %param.21) | copy-start | bytes 7684
  83.7 3.2 copy-start.1
  790.5 3.2 copy-start
Sparse Core Ops, SparseCore 0:
  10.8 101.6 all-gather.4
  115.3 148.1 all-gather.6

commit v2 on v0

v2 whole, which is shorter than its diff:
```python
import functools
import types

import jax
import jax.numpy as jnp
from jax import lax
from jax.experimental import pallas as pl
from jax.experimental.pallas import tpu as pltpu
from jax.sharding import PartitionSpec as P

MESH = pl.DeviceIdType.MESH
BF16 = jnp.bfloat16
F32 = jnp.float32
DMA = pltpu.SemaphoreType.DMA
HEAD_DIM = 128
HEADS = 5
BLOCK = 1024
BLOCKS = 8
COLUMN = 4
WIDTH = 2560
FFN = 1728
WINDOW_BLOCKS = 4
CHUNK = 128
SLICE = 16
ROWS = 256
PIECE = 32
SKEW = 2
TAIL = (32, 32, 16, 16, 16, 16)
TAIL_SKEW = 3
TILE_Q = 512
EXP_SCALE = HEAD_DIM ** -0.5 * 1.4426950408889634
MASKED = -1e30
VMEM_LIMIT = 67_043_328
FULL_SHAPE = (HEADS, COLUMN - 1, BLOCKS, SLICE, WIDTH)
PARAMS = functools.partial(pltpu.CompilerParams, vmem_limit_bytes=VMEM_LIMIT, has_side_effects=True)


def hbm():
    return pl.BlockSpec(memory_space=pl.ANY)


def vmem():
    return pl.BlockSpec(memory_space=pltpu.VMEM)


def bf16(*shape):
    return jax.ShapeDtypeStruct(shape, BF16)


def vmem_bf16(*shape):
    return pltpu.VMEM(shape, BF16)


def vmem_f32(*shape):
    return pltpu.VMEM(shape, F32)


def cost(flops):
    return pl.CostEstimate(flops=int(flops), bytes_accessed=int(5e7), transcendentals=0)


def loop(lo, hi):
    def wrap(body):
        def step(i, carry):
            body(i)
            return carry
        lax.fori_loop(lo, hi, step, 0)
    return wrap


def scoped(name):
    def wrap(fn):
        def inner(*args):
            with jax.named_scope(name):
                return fn(*args)
        return inner
    return wrap


def start(copy):
    copy.start()


def wait(copy):
    copy.wait()


def wait_send(copy):
    copy.wait_send()


def rows_of(i, size=ROWS):
    return pl.ds(pl.multiple_of(i * size, size), size)


def lanes_of(i):
    return rows_of(i, HEAD_DIM)


def dot_rows(a, b):
    return lax.dot_general(a, b, (((1,), (1,)), ((), ())), preferred_element_type=F32)


def normalize(rows, gain):
    rows_f = rows.astype(F32)
    variance = jnp.mean(rows_f * rows_f, axis=-1, keepdims=True)
    return (rows_f * lax.rsqrt(variance + 1e-6) * gain).astype(BF16)


def rotate(part, cos, sin):
    return (part * cos + pltpu.roll(part, HEAD_DIM // 2, 1) * sin).astype(BF16)


def remote(src, dst, send, recv, z, cp):
    return pltpu.make_async_remote_copy(
        src_ref=src, dst_ref=dst, send_sem=send, recv_sem=recv, device_id=(z, cp), device_id_type=MESH)


SENDS_TO = ((1, 2), (0, 2, 3), (3, 1, 0), (2, 1))


def is_middle(z):
    return (z == 1) | (z == 2)


def far_end(z):
    return jnp.where(z == 1, 3, 0)


def other_end(z):
    return jnp.where(z == 1, 0, 3)


def on_each(z, fn):
    for me in range(COLUMN):
        pl.when(z == me)(functools.partial(fn, me))


def plane(cp):
    x_dev = cp + 2 - 4 * ((cp // 2) % 2)
    y_dev = cp + 4 - 8 * (cp // 4)
    c_dev = cp + 1 - 2 * (cp % 2)
    d_dev = x_dev + 4 - 8 * (x_dev // 4)
    return x_dev, y_dev, c_dev, d_dev


def signal(z, cp):
    pl.semaphore_signal(pltpu.get_barrier_semaphore(), inc=1, device_id=(z, cp), device_id_type=MESH)


def arrive(count):
    pl.semaphore_wait(pltpu.get_barrier_semaphore(), count)


def greet_column(z, cp):
    for step in range(1, COLUMN):
        signal(lax.rem(z + step, COLUMN), cp)


def greet_plane(z, cp):
    for other in plane(cp)[:3]:
        signal(z, other)


class ColumnGather:
    def __init__(self, z, cp, part, landing, send, recv):
        self.z, self.cp, self.part, self.landing, self.send, self.recv = z, cp, part, landing, send, recv

    def copy(self, me, target):
        return remote(self.part(me, target), self.landing(me, target), self.send.at[target], self.recv.at[me], target, self.cp)

    def forward(self):
        far, target = far_end(self.z), other_end(self.z)
        return remote(self.landing(far, self.z), self.landing(far, target), self.send.at[COLUMN], self.recv.at[far],
                      target, self.cp)

    def received(self, src):
        ref = self.landing(src, self.z)
        remote(ref, ref, self.send.at[COLUMN], self.recv.at[src], self.z, self.cp).wait_recv()

    def each(self, action):
        def fn(me):
            for target in SENDS_TO[me]:
                action(self.copy(me, target))
        on_each(self.z, fn)

    def begin(self):
        self.each(start)

    def passing(self):
        @pl.when(is_middle(self.z))
        def _():
            self.received(far_end(self.z))
            self.forward().start()

    def finish(self):
        def fn(me):
            for src in range(COLUMN):
                if src != me and not (me in (1, 2) and abs(src - me) == 2):
                    self.received(src)
        on_each(self.z, fn)

    def drain(self):
        self.each(wait_send)

        @pl.when(is_middle(self.z))
        def _():
            self.forward().wait_send()


def column_sems(*lead):
    return [DMA((*lead, COLUMN + 1)), DMA((*lead, COLUMN))]


class PlaneExchange:
    OWN, FROM_X, FROM_Y, FROM_D, COPIES = range(6), range(6, 9), range(9, 12), range(12, 14), 14

    def __init__(self, z, cp, ref, send, recv, own_src=None):
        self.z, self.cp, self.ref, self.send, self.recv = z, cp, ref, send, recv
        self.own_src = own_src or (lambda item, part: ref(item, part, cp))
        x_dev, y_dev, c_dev, d_dev = plane(cp)
        self.routes = [(part, cp, dev) for dev in (x_dev, y_dev, c_dev) for part in range(2)]
        self.routes += [(0, x_dev, y_dev), (0, x_dev, c_dev), (1, x_dev, c_dev)]
        self.routes += [(1, y_dev, x_dev), (0, y_dev, c_dev), (1, y_dev, c_dev)]
        self.routes += [(0, d_dev, c_dev), (1, d_dev, c_dev)]

    def copy(self, item, slot):
        part, block, dev = self.routes[slot]
        dst = self.ref(item, part, block)
        src = self.own_src(item, part) if slot in self.OWN else dst
        return remote(src, dst, self.send.at[item, slot], self.recv.at[item, slot], self.z, dev)

    def group(self, item, slots, action=start):
        for slot in slots:
            action(self.copy(item, slot))

    def arrivals(self, item, slots, block):
        for slot in slots:
            ref = self.ref(item, self.routes[slot][0], block)
            remote(ref, ref, self.send.at[item, slot], self.recv.at[item, slot], self.z, plane(self.cp)[2]).wait_recv()

    def own(self, item, action=start):
        self.group(item, self.OWN, action)

    @scoped("near")
    def near(self, item):
        x_dev, y_dev, _, _ = plane(self.cp)
        self.arrivals(item, self.OWN[:2], x_dev)
        self.group(item, self.FROM_X)
        self.arrivals(item, self.OWN[2:4], y_dev)
        self.group(item, self.FROM_Y)

    @scoped("diagonal")
    def diagonal(self, item):
        d_dev = plane(self.cp)[3]
        for passed, slots in ((self.FROM_X, self.FROM_D[:1]), (self.FROM_Y, self.FROM_D[1:])):
            self.arrivals(item, passed[:1], d_dev)
            self.group(item, slots)

    @scoped("core")
    def core(self, item):
        x_dev, y_dev, c_dev, d_dev = plane(self.cp)
        for slots, block in ((self.OWN[4:], c_dev), (self.FROM_X[1:], self.mate(x_dev)),
                             (self.FROM_Y[1:], self.mate(y_dev)), (self.FROM_D, self.mate(d_dev))):
            self.arrivals(item, slots, block)

    @staticmethod
    def mate(dev):
        return plane(dev)[2]

    def drain(self, item, own=True):
        if own:
            self.own(item, wait_send)
        for slots in (self.FROM_X, self.FROM_Y, self.FROM_D):
            self.group(item, slots, wait_send)


def plane_sems(items):
    return [DMA((items, PlaneExchange.COPIES))] * 2


def weight_slices(layer, z, cp, src, full, send, recv):
    def landing(me, target):
        return full.at[:, lax.rem(me - target + COLUMN, COLUMN) - 1, cp]
    return ColumnGather(z, cp, lambda me, target: src.at[layer, :, cp], landing, send, recv)


def weight_exchange(group, z, cp, full, send, recv):
    half = SLICE // 2

    def ref(item, part, block):
        return full.at[pl.ds(item * group, group), :, block, part * half:(part + 1) * half]
    return PlaneExchange(z, cp, ref, send, recv)


ATTENTION_SCRATCH = [
    vmem_bf16(BLOCK, WIDTH),
    vmem_bf16(HEADS, BLOCK, HEAD_DIM),
    vmem_bf16(HEADS, BLOCK, COLUMN * HEAD_DIM),
    vmem_f32(BLOCK, WIDTH),
    vmem_bf16(2, COLUMN, BLOCKS, SLICE, WIDTH),
    vmem_f32(1, TILE_Q),
    vmem_f32(1, TILE_Q),
    vmem_f32(HEAD_DIM, TILE_Q),
    vmem_f32(BLOCK, TILE_Q),
    vmem_f32(BLOCK, TILE_Q),
    DMA((BLOCK // ROWS,)), DMA((2, COLUMN)), DMA((BLOCK // ROWS,)),
] + column_sems(HEADS, 2)
TILES = BLOCK // TILE_Q


def attention_parts(layer, windowed, z, cp, k_buf, v_buf, slot_of, x_ref, wo_ref, full_ref, out_ref,
                    xh, q_buf, o_all, acc, wo_buf, m_s, l_s, a_s, s0, s1, x_sem, wo_sem, out_sem, o_send, o_recv):
    def load_x(i):
        return pltpu.make_async_copy(x_ref.at[rows_of(i), :], xh.at[rows_of(i), :], x_sem.at[i])

    def gather(h, t):
        def part(me, target):
            return o_all.at[h, rows_of(t, TILE_Q), lanes_of(me)]
        return ColumnGather(z, cp, part, part, o_send.at[h, t], o_recv.at[h, t])

    def o_pass(h):
        for t in range(TILES):
            gather(h, t).passing()

    key_iota = lax.broadcasted_iota(jnp.int32, (BLOCK, TILE_Q), 0)
    row_iota = lax.broadcasted_iota(jnp.int32, (BLOCK, TILE_Q), 1)

    @scoped("attend")
    def attend(h, t):
        q = q_buf[h, rows_of(t, TILE_Q), :]
        ks, vs = k_buf.at[slot_of(h)], v_buf.at[slot_of(h)]

        def scores(j):
            return dot_rows(ks[j], q)

        def soft(s, j, first=False):
            m_new = jnp.max(s, axis=0, keepdims=True)
            if not first:
                m_old = m_s[...]
                m_new = jnp.maximum(m_old, m_new)
                alpha = jnp.exp2((m_old - m_new) * EXP_SCALE)
            p = jnp.exp2((s - m_new) * EXP_SCALE)
            norm = jnp.sum(p, axis=0, keepdims=True)
            out = jnp.dot(vs[j], p.astype(BF16), preferred_element_type=F32)
            l_s[...] = norm if first else l_s[...] * alpha + norm
            a_s[...] = out if first else a_s[...] * alpha + out
            m_s[...] = m_new

        lo = jnp.maximum(cp - (WINDOW_BLOCKS - 1), 0) if windowed else 0
        count = cp - lo
        s0[...] = scores(cp)
        s1[...] = scores(jnp.minimum(lo, cp))
        soft(jnp.where(key_iota <= row_iota + t * TILE_Q, s0[...], MASKED), cp, True)

        @loop(0, count // 2)
        def _(i):
            j = lo + 2 * i
            s0[...] = scores(j + 1)
            soft(s1[...], j)
            s1[...] = scores(jnp.minimum(j + 2, cp))
            soft(s0[...], j + 1)

        @pl.when(count % 2 == 1)
        def _():
            soft(s1[...], cp - 1)

        if windowed:
            @pl.when(cp >= WINDOW_BLOCKS)
            def _():
                edge = cp - WINDOW_BLOCKS
                soft(jnp.where(key_iota > row_iota + t * TILE_Q, scores(edge), MASKED), edge)

        o_all[h, rows_of(t, TILE_Q), lanes_of(z)] = (a_s[...] / l_s[...]).T.astype(BF16)

    def load_wo(h, action=start):
        slot = h % 2
        for part in range(COLUMN):
            rel = lax.rem(part - z + COLUMN, COLUMN)

            def load(src):
                action(pltpu.make_async_copy(src, wo_buf.at[slot, part], wo_sem.at[slot, part]))
            pl.when(rel == 0)(lambda: load(wo_ref.at[layer, h]))
            pl.when(rel > 0)(lambda: load(full_ref.at[h, rel - 1]))

    def store_out(i):
        return pltpu.make_async_copy(xh.at[rows_of(i), :], out_ref.at[rows_of(i), :], out_sem.at[i])

    @scoped("apply_wo")
    def apply_wo(h):
        for t in range(TILES):
            gather(h, t).finish()
        load_wo(h, wait)

        @loop(0, BLOCK // ROWS)
        def _(i):
            rows = rows_of(i)
            weight = wo_buf[h % 2].reshape(COLUMN * HEAD_DIM, WIDTH)
            part = jnp.dot(o_all[h, rows, :], weight, preferred_element_type=F32)

            @pl.when(h == 0)
            def _():
                acc[rows, :] = part

            @pl.when((h > 0) & (h < HEADS - 1))
            def _():
                acc[rows, :] += part

            @pl.when(h == HEADS - 1)
            def _():
                load_x(i).wait()
                xh[rows, :] = (xh[rows, :].astype(F32) + (acc[rows, :] + part)).astype(BF16)
                store_out(i).start()

    def start_x():
        for i in range(BLOCK // ROWS):
            load_x(i).start()

    def drain(h):
        for t in range(TILES):
            gather(h, t).drain()

    def settle():
        for i in range(BLOCK // ROWS):
            store_out(i).wait()

    return types.SimpleNamespace(
        load_x=load_x, start_x=start_x, attend=attend, o_start=lambda h, t: gather(h, t).begin(), o_pass=scoped("o_pass")(o_pass),
        load_wo=load_wo, apply_wo=apply_wo, drain=drain, settle=settle)


def first_kernel(x_ref, gain_ref, wq_ref, wk_ref, wv_ref, bias_ref, cos_ref, sin_ref, wo_ref,
                 out_ref, k_out, v_out, full_ref, next_ref,
                 w_buf, k_buf, v_buf, v_nat, w_sem, kv_sem, send_sem, recv_sem, *rest):
    z = lax.axis_index("tp")
    cp = lax.axis_index("cp")
    count = len(ATTENTION_SCRATCH)
    xh, q_buf = rest[:2]
    z_send, z_recv, n_send, n_recv, p_send, p_recv = rest[count:]
    slices = weight_slices(0, z, cp, wo_ref, full_ref, z_send, z_recv)
    next_slices = weight_slices(1, z, cp, wo_ref, next_ref, n_send, n_recv)
    weights = weight_exchange(1, z, cp, full_ref, p_send, p_recv)
    kv = PlaneExchange(z, cp, lambda h, part, block: (k_buf, v_buf)[part].at[h, block], send_sem, recv_sem)
    parts = attention_parts(0, False, z, cp, k_buf, v_buf, lambda h: h, x_ref, wo_ref, full_ref, out_ref, *rest[:count])

    def load_w(h, action):
        slot = h % 2
        for i, w in enumerate((wq_ref, wk_ref, wv_ref)):
            action(pltpu.make_async_copy(w.at[0, :, lanes_of(h)], w_buf.at[slot, :, lanes_of(i)], w_sem.at[slot, i]))

    greet_plane(z, cp)
    greet_column(z, cp)
    parts.start_x()
    load_w(0, start)
    arrive(6)
    slices.begin()
    next_slices.begin()
    gain = gain_ref[:1, :].astype(F32)

    @loop(0, BLOCK // ROWS)
    def _(i):
        parts.load_x(i).wait()
        xh[rows_of(i), :] = normalize(xh[rows_of(i), :], gain)

    def caches(h, action):
        action(pltpu.make_async_copy(k_buf.at[h, cp], k_out.at[h], kv_sem.at[h, 0]))
        action(pltpu.make_async_copy(v_nat.at[h], v_out.at[h], kv_sem.at[h, 1]))

    @loop(0, HEADS)
    @scoped("project")
    def _(h):
        @pl.when(h + 1 < HEADS)
        def _():
            load_w(h + 1, start)
        load_w(h, wait)

        @loop(0, BLOCK // ROWS)
        def _(i):
            rows = rows_of(i)
            proj = jnp.dot(xh[rows, :], w_buf[h % 2], preferred_element_type=F32)
            q, k, v = (proj[:, n * HEAD_DIM:(n + 1) * HEAD_DIM] + bias_ref[h, n:n + 1, :].astype(F32) for n in range(3))
            cos = cos_ref[rows, :]
            sin = sin_ref[rows, :]
            q_buf[h, rows, :] = rotate(q, cos, sin)
            k_buf[h, cp, rows, :] = rotate(k, cos, sin)
            v_nat[h, rows, :] = v.astype(BF16)
            v_buf[h, cp, :, rows] = v.T.astype(BF16)

        @pl.when(h == 0)
        def _():
            kv.own(0)

        @pl.when(h == 3)
        def _():
            kv.near(0)
            kv.own(1)
            kv.own(2)
        caches(h, start)

    slices.passing()
    kv.diagonal(0)
    parts.start_x()

    def between(h):
        @pl.when(h + 1 < HEADS)
        def _():
            kv.near(h + 1)

        @pl.when(h + 3 < HEADS)
        def _():
            kv.own(h + 3)

        @pl.when(h == HEADS - 2)
        def _():
            slices.finish()
            weights.own(0)
            weights.own(1)

        @pl.when(h == HEADS - 1)
        def _():
            weights.near(0)
            weights.own(2)

    def behind(h):
        pl.when(h == 0)(next_slices.passing)
        pl.when(h + 1 < HEADS)(lambda: kv.diagonal(h + 1))
        pl.when(h >= 1)(lambda: parts.o_pass(h - 1))

    @loop(0, HEADS * TILES)
    def _(i):
        h, t = i // TILES, i % TILES
        pl.when(t == 0)(lambda: kv.core(h))
        parts.attend(h, t)
        parts.o_start(h, t)
        pl.when(t == 0)(lambda: between(h))
        pl.when(t == TILES - 1)(lambda: behind(h))

    weights.near(1)
    weights.own(3)

    @loop(0, HEADS)
    def _(h):
        weights.diagonal(h)
        weights.core(h)
        parts.load_wo(h)

        @pl.when(h + 2 < HEADS)
        def _():
            weights.near(h + 2)

        @pl.when(h == 0)
        def _():
            weights.own(4)

        @pl.when(h == 2)
        def _():
            parts.o_pass(HEADS - 1)
        parts.apply_wo(h)

    @loop(0, HEADS)
    def _(h):
        kv.drain(h)
        weights.drain(h)
        caches(h, wait)
        parts.drain(h)

    next_slices.finish()
    next_slices.drain()
    slices.drain()
    parts.settle()


def first_call(*args):
    return pl.pallas_call(
        first_kernel,
        out_shape=(bf16(BLOCK, WIDTH), bf16(HEADS, BLOCK, HEAD_DIM), bf16(HEADS, BLOCK, HEAD_DIM),
                   bf16(*FULL_SHAPE), bf16(*FULL_SHAPE)),
        in_specs=[hbm(), vmem(), hbm(), hbm(), hbm(), vmem(), vmem(), vmem(), hbm()],
        out_specs=(hbm(),) * 5,
        scratch_shapes=[
            vmem_bf16(2, WIDTH, 3 * HEAD_DIM),
            vmem_bf16(HEADS, BLOCKS, BLOCK, HEAD_DIM),
            vmem_bf16(HEADS, BLOCKS, HEAD_DIM, BLOCK),
            vmem_bf16(HEADS, BLOCK, HEAD_DIM),
            DMA((2, 3)), DMA((HEADS, 2)),
        ] + plane_sems(HEADS) + ATTENTION_SCRATCH + column_sems() + column_sems() + plane_sems(HEADS),
        compiler_params=PARAMS(collective_id=1),
        cost_estimate=cost(7e10),
        name="front0",
    )(*args)


def second_kernel(x_ref, q_ref, k_ref, v_ref, wo_ref, full_ref, out_ref, k_buf, v_buf, q_sem, kv_sem, *rest):
    z = lax.axis_index("tp")
    cp = lax.axis_index("cp")
    parts = attention_parts(
        1, True, z, cp, k_buf, v_buf, lambda h: h % 2, x_ref, wo_ref, full_ref, out_ref, *rest)

    def load_kv(h, action):
        slot = h % 2
        for i, (src, dst) in enumerate(((k_ref, k_buf), (v_ref, v_buf))):
            action(pltpu.make_async_copy(src.at[h], dst.at[slot], kv_sem.at[slot, i]))

    greet_column(z, cp)
    load_q = pltpu.make_async_copy(q_ref, rest[1], q_sem)
    load_q.start()
    load_kv(0, start)
    load_q.wait()
    lag = 2

    def ahead(h):
        load_kv(h, wait)
        pl.when(h + 1 < HEADS)(lambda: load_kv(h + 1, start))

    def behind(h):
        pl.when(h >= 1)(lambda: parts.o_pass(h - 1))

        @pl.when(h >= lag)
        def _():
            parts.load_wo(h - lag + 1)
            parts.apply_wo(h - lag)

    @loop(0, HEADS * TILES)
    def _(i):
        h, t = i // TILES, i % TILES
        pl.when(t == 0)(lambda: ahead(h))
        parts.attend(h, t)

        @pl.when(i == 0)
        def _():
            arrive(3)
            parts.load_wo(0)
            parts.start_x()
        parts.o_start(h, t)
        pl.when(t == TILES - 1)(lambda: behind(h))

    parts.o_pass(HEADS - 1)

    @loop(HEADS - lag, HEADS)
    def _(h):
        @pl.when(h + 1 < HEADS)
        def _():
            parts.load_wo(h + 1)
        parts.apply_wo(h)

    @loop(0, HEADS)
    def _(h):
        parts.drain(h)
    parts.settle()


def second_call(*args):
    return pl.pallas_call(
        second_kernel,
        out_shape=bf16(BLOCK, WIDTH),
        in_specs=[hbm()] * 6,
        out_specs=hbm(),
        scratch_shapes=[
            vmem_bf16(2, BLOCKS, BLOCK, HEAD_DIM),
            vmem_bf16(2, BLOCKS, HEAD_DIM, BLOCK),
            DMA, DMA((2, 2)),
        ] + ATTENTION_SCRATCH,
        compiler_params=PARAMS(collective_id=2),
        cost_estimate=cost(5e10),
        name="front1",
    )(*args)


CHUNKS = BLOCK // CHUNK
PER_CHUNK = CHUNK // PIECE
REGULAR = (CHUNKS - 1) * PER_CHUNK


def mlp_kernel(layer, *refs):
    following = layer == 0
    x_ref, gain_ref, wg_ref, wu_ref, wd_ref, *refs = refs
    if following:
        next_gain, wq_ref, wk_ref, wv_ref, bias_ref, cos_ref, sin_ref, _, *refs = refs
        out_ref, q_out, k_out, v_out, k_all, v_all, full_ref, *refs = refs
    else:
        out_ref, *refs = refs
    wg, wu, wd, xv, pv, rv, sv, act, load_sem, r_send, r_recv, s_send, s_recv, x_send, x_recv, x_local, *refs = refs
    z = lax.axis_index("tp")
    cp = lax.axis_index("cp")
    inner = is_middle(z)
    outer = jnp.logical_not(inner)
    partner = z + 1 - 2 * (z % 2)
    middle = jnp.where(inner, 3 - z, z)
    tail = [(BLOCK - CHUNK + sum(TAIL[:i]), size, REGULAR + i) for i, size in enumerate(TAIL)]

    load_x, load_g, load_u, load_d = (
        pltpu.make_async_copy(src, dst, load_sem.at[i]) for i, (src, dst) in enumerate((
            (x_ref, xv), (wg_ref.at[layer], wg), (wu_ref.at[layer], wu), (wd_ref.at[layer], wd))))
    load_x.start()
    load_g.start()

    signal(partner, cp)
    pl.when(inner)(lambda: signal(middle, cp))
    if following:
        w_buf, q_st, k_st, v_st, n_st, w_sem, st_sem, send_sem, recv_sem, p_send, p_recv = refs
        greet_plane(z, cp)
        weights = weight_exchange(HEADS, z, cp, full_ref, p_send, p_recv)
    pl.when(inner)(lambda: arrive(5 if following else 2))
    pl.when(outer)(lambda: arrive(4 if following else 1))

    gain = gain_ref[layer:layer + 1, :].astype(F32)
    load_x.wait()

    def chunk_rows(j):
        return rows_of(j, CHUNK)

    def piece(i):
        return pl.multiple_of(i * PIECE, PIECE), PIECE, i

    def piece_copy(src, dst, send, recv, part, dev):
        at, size, i = part
        return remote(src.at[pl.ds(at, size), :], dst.at[pl.ds(at, size), :], send.at[i], recv.at[i], dev, cp)

    def copy_r(part):
        return piece_copy(pv, rv, r_send, r_recv, part, partner)

    def copy_s(part):
        return piece_copy(pv, sv, s_send, s_recv, part, middle)

    def copy_x(part):
        return piece_copy(xv, xv if following else out_ref, x_send, x_recv, part, partner)

    def copy_local(part):
        at, size, i = part
        return pltpu.make_async_copy(xv.at[pl.ds(at, size), :], out_ref.at[pl.ds(at, size), :], x_local.at[i])

    @scoped("activate")
    def activate(j):
        normed = normalize(xv[chunk_rows(j), :], gain)

        @pl.when(j == 0)
        def _():
            load_g.wait()
            load_u.start()
            load_d.start()
        gate = dot_rows(normed, wg[...])
        pl.when(j == 0)(load_u.wait)
        up = dot_rows(normed, wu[...])
        act[...] = (gate * jax.nn.sigmoid(gate) * up).astype(BF16)

    @scoped("down")
    def down(j):
        pl.when(j == 0)(load_d.wait)
        pv[chunk_rows(j), :] = jnp.dot(act[...], wd[...], preferred_element_type=F32).astype(BF16)

    @scoped("add_end")
    def add_end(part):
        rows = pl.ds(part[0], part[1])
        copy_r(part).wait_recv()
        pv[rows, :] = (pv[rows, :].astype(F32) + rv[rows, :].astype(F32)).astype(BF16)
        copy_s(part).start()

    @scoped("add_middle")
    def add_middle(part):
        rows = pl.ds(part[0], part[1])
        copy_s(part).wait_recv()
        total = pv[rows, :].astype(F32) + sv[rows, :].astype(F32)
        xv[rows, :] = (xv[rows, :].astype(F32) + total).astype(BF16)
        copy_x(part).start()
        copy_local(part).start()

    if following:
        load_w = [
            pltpu.make_async_copy(w.at[layer + 1], w_buf.at[i], w_sem.at[i])
            for i, w in enumerate((wq_ref, wk_ref, wv_ref))]
        gain_n = next_gain[layer + 1:layer + 2, :].astype(F32)

        def kv_ref(c, part, block):
            rows = chunk_rows(c)
            return v_all.at[:, block, :, rows] if part else k_all.at[:, block, rows, :]
        kv = PlaneExchange(z, cp, kv_ref, send_sem, recv_sem, lambda c, part: (k_st, v_st)[part].at[c % 2])

        def stores(c, action):
            rows = chunk_rows(c)
            slot = c % 2
            for i, (src, dst) in enumerate((
                    (q_st, q_out.at[:, rows, :]), (k_st, k_out.at[:, rows, :]), (n_st, v_out.at[:, rows, :]),
                    (k_st, kv_ref(c, 0, cp)), (v_st, kv_ref(c, 1, cp)))):
                action(pltpu.make_async_copy(src.at[slot], dst, st_sem.at[slot, i]))

        @scoped("x_wait")
        def x_wait(c):
            def land(parts):
                for part in parts:
                    copy_x(part).wait_recv()
                    copy_local(part).start()
            pl.when(outer & (c < CHUNKS - 1))(lambda: land([piece(c * PER_CHUNK + k) for k in range(PER_CHUNK)]))
            pl.when(outer & (c == CHUNKS - 1))(lambda: land(tail))

        def project(c):
            x_wait(c)
            pl.when(c >= 1)(lambda: kv.near(c - 1))

            @pl.when(c >= 2)
            def _():
                kv.diagonal(c - 2)
                kv.own(c - 2, wait_send)
                stores(c - 2, wait)

            with jax.named_scope("project"):
                rows = chunk_rows(c)
                slot = c % 2
                normed = normalize(xv[rows, :], gain_n)
                cos = cos_ref[rows, :]
                sin = sin_ref[rows, :]
                for which in range(3):
                    proj = jnp.dot(normed, w_buf[which], preferred_element_type=F32)
                    for h in range(HEADS):
                        part = proj[:, h * HEAD_DIM:(h + 1) * HEAD_DIM] + bias_ref[h, which:which + 1, :].astype(F32)
                        if which < 2:
                            (q_st, k_st)[which][slot, h] = rotate(part, cos, sin)
                        else:
                            n_st[slot, h] = part.astype(BF16)
                            v_st[slot, h] = part.T.astype(BF16)
            kv.own(c)
            stores(c, start)

    def serve(j, half):
        @loop(0, PER_CHUNK // 2)
        def _(k):
            i = j * PER_CHUNK + half * (PER_CHUNK // 2) + k
            add_end(piece(i))
            pl.when(i >= SKEW)(lambda: add_middle(piece(i - SKEW)))

    def serve_tail(first, last):
        for i in range(first, last):
            if i < len(tail):
                add_end(tail[i])
            if i == 0:
                for k in range(SKEW, 0, -1):
                    add_middle(piece(REGULAR - k))
            elif i >= TAIL_SKEW:
                add_middle(tail[i - TAIL_SKEW])

    tail_end = len(tail) + TAIL_SKEW
    lag = jnp.where(inner, 2, 5)

    @loop(0, CHUNKS)
    def _(j):
        activate(j)
        pl.when(inner & (j >= 1))(lambda: serve(j - 1, 0))
        down(j)

        @pl.when(outer & (j < CHUNKS - 1))
        def _():
            for k in range(PER_CHUNK):
                copy_r(piece(j * PER_CHUNK + k)).start()

        @pl.when(outer & (j == CHUNKS - 1))
        def _():
            for part in tail:
                copy_r(part).start()

        if following:
            @pl.when(j == 0)
            def _():
                weights.own(0)
                for copy in load_w:
                    copy.start()

            @pl.when(j == 1)
            def _():
                for copy in load_w:
                    copy.wait()
            pl.when(j == jnp.where(inner, 2, 3))(lambda: weights.near(0))
            pl.when(j == 5)(lambda: weights.diagonal(0))
            pl.when(j == 6)(lambda: weights.core(0))
            pl.when(j >= lag)(lambda: project(j - lag))
        pl.when(inner & (j >= 1))(lambda: serve(j - 1, 1))

    if following:
        @loop(CHUNKS - lag, CHUNKS)
        def _(c):
            pl.when(inner & (c == CHUNKS - 2))(lambda: serve_tail(0, 1))
            pl.when(inner & (c == CHUNKS - 1))(lambda: serve_tail(1, tail_end))
            project(c)
        kv.near(CHUNKS - 1)
        kv.diagonal(CHUNKS - 2)
        kv.diagonal(CHUNKS - 1)

        @loop(0, CHUNKS)
        def _(c):
            kv.core(c)
            kv.drain(c, False)

            @pl.when(c >= CHUNKS - 2)
            def _():
                kv.own(c, wait_send)
                stores(c, wait)
        weights.drain(0)
    else:
        pl.when(inner)(lambda: serve_tail(0, tail_end))

    def drain(part):
        @pl.when(inner)
        def _():
            copy_s(part).wait_send()
            copy_x(part).wait_send()
            copy_local(part).wait()

        @pl.when(outer)
        def _():
            copy_r(part).wait_send()
            if following:
                copy_local(part).wait()
            else:
                copy_x(part).wait_recv()

    @loop(0, REGULAR)
    def _(i):
        drain(piece(i))
    for part in tail:
        drain(part)


def mlp_call(layer, *args):
    outs = [bf16(BLOCK, WIDTH)]
    in_specs = [hbm(), vmem(), hbm(), hbm(), hbm()]
    scratch = [vmem_bf16(FFN, WIDTH)] * 3 + [vmem_bf16(BLOCK, WIDTH)] * 4 + [vmem_bf16(CHUNK, FFN), DMA((COLUMN,))]
    scratch += [DMA((REGULAR + len(TAIL),))] * 7
    aliases = {}
    if layer == 0:
        outs += [bf16(HEADS, BLOCK, HEAD_DIM)] * 3
        outs += [bf16(HEADS, BLOCKS, BLOCK, HEAD_DIM), bf16(HEADS, BLOCKS, HEAD_DIM, BLOCK), bf16(*FULL_SHAPE)]
        in_specs += [vmem(), hbm(), hbm(), hbm(), vmem(), vmem(), vmem(), hbm()]
        aliases = {len(in_specs) - 1: len(outs) - 1}
        scratch += [vmem_bf16(3, WIDTH, HEADS * HEAD_DIM)] + [vmem_bf16(2, HEADS, CHUNK, HEAD_DIM)] * 4
        scratch += [DMA((3,)), DMA((2, 5))] + plane_sems(CHUNKS) + plane_sems(1)
    return pl.pallas_call(
        functools.partial(mlp_kernel, layer),
        out_shape=tuple(outs),
        in_specs=in_specs,
        out_specs=(hbm(),) * len(outs),
        scratch_shapes=scratch,
        input_output_aliases=aliases,
        compiler_params=PARAMS(collective_id=3 + layer),
        cost_estimate=cost(1e11),
        name=f"mlp{layer}",
    )(*args)


def solution(mesh):
    def local_step(x_in, positions, attn_gain, mlp_gain, w_query, b_query, w_key, b_key, w_value, b_value,
                   w_out, w_gate, w_up, w_down):
        inv_freq = 1.0 / (1000000.0 ** (jnp.arange(0, HEAD_DIM, 2, dtype=F32) / HEAD_DIM))
        angles = positions.astype(F32)[:, None] * inv_freq[None, :]
        cos, sin = jnp.cos(angles), jnp.sin(angles)
        cos = jnp.concatenate([cos, cos], axis=1)
        sin = jnp.concatenate([-sin, sin], axis=1)

        w_gate = jnp.swapaxes(w_gate, 1, 2)
        w_up = jnp.swapaxes(w_up, 1, 2)
        wo = w_out.reshape(2, HEADS, BLOCKS, SLICE, WIDTH)
        bias = [jnp.stack([b.reshape(2, HEADS, HEAD_DIM)[layer] for b in (b_query, b_key, b_value)], axis=1)
                for layer in range(2)]
        hidden, k0, v0, _, full1 = first_call(x_in, attn_gain, w_query, w_key, w_value, bias[0], cos, sin, wo)
        hidden, q, k1, v1, k_all, v_all, full1 = mlp_call(
            0, hidden, mlp_gain, w_gate, w_up, w_down, attn_gain, w_query, w_key, w_value, bias[1], cos, sin, full1)
        hidden = second_call(hidden, q, k_all, v_all, wo, full1)
        hidden, = mlp_call(1, hidden, mlp_gain, w_gate, w_up, w_down)
        return (hidden,) + tuple(jnp.swapaxes(cache, 0, 1) for cache in (k0, v0, k1, v1))

    weight_col = P(None, None, "tp")
    bias_col = P(None, "tp")
    weight_row = P(None, "tp", None)
    replicated = P(None, None)
    cache_spec = P("cp", "tp", None)
    in_specs = (P("cp", None), P("cp"), replicated, replicated, weight_col, bias_col, weight_col, bias_col,
                weight_col, bias_col, weight_row, weight_col, weight_col, weight_row)
    out_specs = (P("cp", None), cache_spec, cache_spec, cache_spec, cache_spec)
    return jax.shard_map(local_step, mesh=mesh, in_specs=in_specs, out_specs=out_specs, check_vma=False)
```

time: 1880 us -> 603 us (0.32)
  waiting for transfers between devices: 981 us -> 0 us
  Pallas kernels: 0 us -> 586 us
  matrix products: 578 us -> 0 us
  other arithmetic: 241 us -> 4.53 us
  local copies, waits for them, and re-layouts: 50.7 us -> 11.9 us
    psum x4 -> x0, waiting for transfers between devices: 748 us -> none  [the longest x2 375 us: local_step(): lax.psum(attn_part, 'tp').astype(jnp.float32)]
    pallas_call x0 -> x4, Pallas kernels: none -> 586 us  [the longest x2 324 us: mlp_call(): pl.pallas_call(functools.partial(mlp_kernel, layer), out_shape=tuple(outs...]
    dot_general x44 -> x0, matrix products: 578 us -> none  [the longest x16 213 us: one_block(): jnp.einsum('qkgs,skd->qkgd', probs_bf, value_all, preferred_element_type=...]
    all_gather x4 -> x0, waiting for transfers between devices: 233 us -> none  [the longest x2 131 us: local_step(): value_all = lax.all_gather(value_cache, 'cp', axis=0, tiled=True)]
    reduce_sum x20 -> x0, other arithmetic: 190 us -> none  [the longest x16 164 us: one_block(): probs_bf = jax.nn.softmax(scores, axis=-1).astype(jnp.bfloat16)]
  transfers between devices with their start and end apart: 8 -> 0, of which waited for: 8 -> 0; matrix products, arithmetic and copies ran while one was open for 1% -> 0% of each run, Pallas kernels for 0% -> 0%
where the time goes in v2:
time: 603 us
  Pallas kernels  586 us (97%)
  local copies, waits for them, and re-layouts  11.9 us (2%)
    pallas_call x2, Pallas kernels, mlp_call(): pl.pallas_call(functools.partial(mlp_kernel, layer), out_shape=tuple(outs...  324 us
    pallas_call x1, Pallas kernels, first_call(): pl.pallas_call(first_kernel, out_shape=(bf16(BLOCK, WIDTH), bf16(HEADS, B...  166 us
    pallas_call x1, Pallas kernels, second_call(): pl.pallas_call(second_kernel, out_shape=bf16(BLOCK, WIDTH), in_specs=[hbm...  95.1 us

profile of v2, /device:TPU:0, one launch (start us, length us, event | category | flops | bytes accessed | tf_op | source)
XLA Modules:
  0.0 602.7 jit_solution(15023423851688718416)
XLA Ops:
  0.6 0.7 convert_element_type.3
  1.3 0.8 slice_bitcast_fusion.2
  2.1 0.8 slice_bitcast_fusion.1
  2.9 0.8 slice_bitcast_fusion
  3.6 0.6 pad_maximum_fusion.2
  4.3 1.9 fusion
  6.2 1.3 pad_maximum_fusion
  7.5 166.1 %front0.1 = (bf16[1024,2560]{1,0:T(8,128)(2,1)}, bf16[5,1024,128]{2,1,0:T(8,128)(2,1)}, bf16[5,1024,128]{2,1,0:T(8,128)(2,1)}, bf16[5,3,8,16,2560]{4,3,2,1,0:T(8,128)(2,1)}, bf16[5,3,8,16,2560]{4,3,2,1,0:T(8,128)(2,1)}) custom-call(bf16[1024,2560]{1,0:T(8,128)(2,1)} %x_ref.1, bf16[2,2560]{1,0:T(2,128)(2,1)} %refs_5_.1, bf16[2,2560,640]{2,1,0:T(8,128)(2,1)} %refs_6_.1, ...), custom_call_target="tpu_custom_call" | custom-call | flops 70000001024 | bytes 50000000 | tf_op jit(solution)/shard_map/front0/pallas_call | solution.py:574
  173.6 178.6 %mlp0.1 = (bf16[1024,2560]{1,0:T(8,128)(2,1)}, bf16[5,1024,128]{2,1,0:T(8,128)(2,1)}, bf16[5,1024,128]{2,1,0:T(8,128)(2,1)}, bf16[5,1024,128]{2,1,0:T(8,128)(2,1...) custom-call(bf16[1024,2560]{1,0:T(8,128)(2,1)} %get-tuple-element.16, ...), custom_call_target="tpu_custom_call", output_to_operand_aliasing={{6}: (12, {})} | custom-call | flops 99999997952 | bytes 50000000 | tf_op jit(solution)/shard_map/mlp0/pallas_call | solution.py:934
  352.2 95.1 %front1.1.refs_0_ = bf16[1024,2560]{1,0:T(8,128)(2,1)} custom-call(bf16[1024,2560]{1,0:T(8,128)(2,1)} %get-tuple-element.18.x_ref, bf16[5,1024,128]{2,1,0:T(8,128)(2,1)} %get-tuple-element.19.q_ref, bf16[5,8,1024,128]{3,2,1,0:T(8,128)(2,1)} %get-tuple-element.20.k_ref, bf16[5,8,128,1024]{3,2,1,0:T(8,128)(2,1)} %get-tuple-element.21.v_ref, ...), custom_call_target="tpu_custom_call" | custom-call | flops 49999998976 | bytes 50000000 | tf_op jit(solution)/shard_map/front1/pallas_call | solution.py:653
  447.2 145.8 %mlp1.1 = bf16[1024,2560]{1,0:T(8,128)(2,1)} custom-call(bf16[1024,2560]{1,0:T(8,128)(2,1)} %front1.1.refs_0_, bf16[2,2560]{1,0:T(2,128)(2,1)} %refs_1_.3, bf16[2,1728,2560]{2,1,0:T(8,128)(2,1)} %bitcast.24, bf16[2,1728,2560]{2,1,0:T(8,128)(2,1)} %bitcast.26, bf16[2,1728,2560]{2,1,0:T(8,128)(2,1)} %refs_4_.3), custom_call_target="tpu_custom_call" | custom-call | flops 99999997952 | bytes 50000000 | tf_op jit(solution)/shard_map/mlp1/pallas_call | solution.py:934
  593.1 0.0 copy-start.1
  593.1 0.0 copy-start
  593.1 0.0 copy-start.3
  593.1 5.4 copy.26
  598.4 0.0 copy-done.1
  598.4 0.0 copy-start.2
  598.4 1.1 copy.27
  599.5 0.0 copy-done
  599.5 1.1 copy.28
  600.6 0.0 copy-done.3
  600.6 1.1 copy.29
  601.6 0.0 copy-done.2
  601.6 1.1 copy.30
  (1 shorter events, 0.0 us)
Async XLA Ops:
  593.1 5.4 copy-start.1
  593.1 6.4 %copy-start = (bf16[5,1024,128]{2,1,0:T(8,128)(2,1)S(1)}, bf16[5,1024,128]{2,1,0:T(8,128)(2,1)}, u32[]{:S(2)}) copy-start(bf16[5,1024,128]{2,1,0:T(8,128)(2,1)} %get-tuple-element.24) | copy-start | bytes 3932164
  593.1 7.5 %copy-start.3 = (bf16[5,1024,128]{2,1,0:T(8,128)(2,1)S(1)}, bf16[5,1024,128]{2,1,0:T(8,128)(2,1)}, u32[]{:S(2)}) copy-start(bf16[5,1024,128]{2,1,0:T(8,128)(2,1)} %get-tuple-element.25) | copy-start | bytes 3932164
  598.4 3.2 copy-start.2

commit v3 on v2

--- a/solution.py
+++ b/solution.py
@@ -25,12 +25,14 @@
 ROWS = 256
 PIECE = 32
 SKEW = 2
+HEAD = (16, 16, 16, 16, 32, 32)
 TAIL = (32, 32, 16, 16, 16, 16)
 TAIL_SKEW = 3
 TILE_Q = 512
 EXP_SCALE = HEAD_DIM ** -0.5 * 1.4426950408889634
 MASKED = -1e30
 VMEM_LIMIT = 67_043_328
+FFN_PARTS = (slice(0, 768), slice(768, FFN))
 FULL_SHAPE = (HEADS, COLUMN - 1, BLOCKS, SLICE, WIDTH)
 PARAMS = functools.partial(pltpu.CompilerParams, vmem_limit_bytes=VMEM_LIMIT, has_side_effects=True)
 
@@ -293,6 +295,8 @@
     return PlaneExchange(z, cp, ref, send, recv)
 
 
+TILES = BLOCK // TILE_Q
+COLS = WIDTH // TILE_Q
 ATTENTION_SCRATCH = [
     vmem_bf16(BLOCK, WIDTH),
     vmem_bf16(HEADS, BLOCK, HEAD_DIM),
@@ -304,9 +308,8 @@
     vmem_f32(HEAD_DIM, TILE_Q),
     vmem_f32(BLOCK, TILE_Q),
     vmem_f32(BLOCK, TILE_Q),
-    DMA((BLOCK // ROWS,)), DMA((2, COLUMN)), DMA((BLOCK // ROWS,)),
+    DMA((BLOCK // ROWS,)), DMA((2, COLUMN)), DMA((COLS,)),
 ] + column_sems(HEADS, 2)
-TILES = BLOCK // TILE_Q
 
 
 def attention_parts(layer, windowed, z, cp, k_buf, v_buf, slot_of, x_ref, wo_ref, full_ref, out_ref,
@@ -384,7 +387,8 @@
             pl.when(rel > 0)(lambda: load(full_ref.at[h, rel - 1]))
 
     def store_out(i):
-        return pltpu.make_async_copy(xh.at[rows_of(i), :], out_ref.at[rows_of(i), :], out_sem.at[i])
+        cols = rows_of(i, TILE_Q)
+        return pltpu.make_async_copy(xh.at[:, cols], out_ref.at[:, cols], out_sem.at[i])
 
     @scoped("apply_wo")
     def apply_wo(h):
@@ -392,24 +396,28 @@
             gather(h, t).finish()
         load_wo(h, wait)
 
-        @loop(0, BLOCK // ROWS)
+        @pl.when(h == HEADS - 1)
+        def _():
+            for i in range(BLOCK // ROWS):
+                load_x(i).wait()
+
+        @loop(0, COLS)
         def _(i):
-            rows = rows_of(i)
-            weight = wo_buf[h % 2].reshape(COLUMN * HEAD_DIM, WIDTH)
-            part = jnp.dot(o_all[h, rows, :], weight, preferred_element_type=F32)
+            cols = rows_of(i, TILE_Q)
+            weight = wo_buf[h % 2, :, :, :, cols].reshape(COLUMN * HEAD_DIM, TILE_Q)
+            part = jnp.dot(o_all[h], weight, preferred_element_type=F32)
 
             @pl.when(h == 0)
             def _():
-                acc[rows, :] = part
+                acc[:, cols] = part
 
             @pl.when((h > 0) & (h < HEADS - 1))
             def _():
-                acc[rows, :] += part
+                acc[:, cols] += part
 
             @pl.when(h == HEADS - 1)
             def _():
-                load_x(i).wait()
-                xh[rows, :] = (xh[rows, :].astype(F32) + (acc[rows, :] + part)).astype(BF16)
+                xh[:, cols] = (xh[:, cols].astype(F32) + (acc[:, cols] + part)).astype(BF16)
                 store_out(i).start()
 
     def start_x():
@@ -421,7 +429,7 @@
             gather(h, t).drain()
 
     def settle():
-        for i in range(BLOCK // ROWS):
+        for i in range(COLS):
             store_out(i).wait()
 
     return types.SimpleNamespace(
@@ -474,9 +482,9 @@
             load_w(h + 1, start)
         load_w(h, wait)
 
-        @loop(0, BLOCK // ROWS)
+        @loop(0, TILES)
         def _(i):
-            rows = rows_of(i)
+            rows = rows_of(i, TILE_Q)
             proj = jnp.dot(xh[rows, :], w_buf[h % 2], preferred_element_type=F32)
             q, k, v = (proj[:, n * HEAD_DIM:(n + 1) * HEAD_DIM] + bias_ref[h, n:n + 1, :].astype(F32) for n in range(3))
             cos = cos_ref[rows, :]
@@ -502,28 +510,24 @@
     parts.start_x()
 
     def between(h):
-        @pl.when(h + 1 < HEADS)
-        def _():
-            kv.near(h + 1)
-
-        @pl.when(h + 3 < HEADS)
-        def _():
-            kv.own(h + 3)
-
-        @pl.when(h == HEADS - 2)
+        pl.when(h == 0)(lambda: kv.near(1))
+        pl.when(h + 3 < HEADS)(lambda: kv.own(h + 3))
+
+        @pl.when(h == HEADS - 1)
+        def _():
+            weights.near(0)
+            weights.own(2)
+
+    def behind(h):
+        pl.when(h == 0)(next_slices.passing)
+        pl.when(h + 1 < HEADS)(lambda: kv.diagonal(h + 1))
+        pl.when(h + 2 < HEADS)(lambda: kv.near(h + 2))
+
+        @pl.when(h == HEADS - 3)
         def _():
             slices.finish()
             weights.own(0)
             weights.own(1)
-
-        @pl.when(h == HEADS - 1)
-        def _():
-            weights.near(0)
-            weights.own(2)
-
-    def behind(h):
-        pl.when(h == 0)(next_slices.passing)
-        pl.when(h + 1 < HEADS)(lambda: kv.diagonal(h + 1))
         pl.when(h >= 1)(lambda: parts.o_pass(h - 1))
 
     @loop(0, HEADS * TILES)
@@ -537,25 +541,18 @@
 
     weights.near(1)
     weights.own(3)
+    weights.diagonal(0)
 
     @loop(0, HEADS)
     def _(h):
-        weights.diagonal(h)
         weights.core(h)
         parts.load_wo(h)
-
-        @pl.when(h + 2 < HEADS)
-        def _():
-            weights.near(h + 2)
-
-        @pl.when(h == 0)
-        def _():
-            weights.own(4)
-
-        @pl.when(h == 2)
-        def _():
-            parts.o_pass(HEADS - 1)
+        pl.when(h + 2 < HEADS)(lambda: weights.near(h + 2))
+        pl.when(h == 0)(lambda: weights.own(4))
+        pl.when(h == 2)(lambda: parts.o_pass(HEADS - 1))
+        pl.when((h >= 1) & (h + 1 < HEADS))(lambda: weights.diagonal(h + 1))
         parts.apply_wo(h)
+        pl.when(h == 0)(lambda: weights.diagonal(1))
 
     @loop(0, HEADS)
     def _(h):
@@ -667,8 +664,9 @@
 
 
 CHUNKS = BLOCK // CHUNK
+HEAD_SLOTS = ((0, 1), (2, 3), (4,), (5,))
 PER_CHUNK = CHUNK // PIECE
-REGULAR = (CHUNKS - 1) * PER_CHUNK
+REGULAR = len(HEAD) + (CHUNKS - 2) * PER_CHUNK
 
 
 def mlp_kernel(layer, *refs):
@@ -679,20 +677,23 @@
         out_ref, q_out, k_out, v_out, k_all, v_all, full_ref, *refs = refs
     else:
         out_ref, *refs = refs
-    wg, wu, wd, xv, pv, rv, sv, act, load_sem, r_send, r_recv, s_send, s_recv, x_send, x_recv, x_local, *refs = refs
+    wg, wu, wd, xv, pv, rv, sv, act, normed, load_sem, r_send, r_recv, s_send, s_recv, x_send, x_recv, x_local, *refs = refs
     z = lax.axis_index("tp")
     cp = lax.axis_index("cp")
     inner = is_middle(z)
     outer = jnp.logical_not(inner)
     partner = z + 1 - 2 * (z % 2)
     middle = jnp.where(inner, 3 - z, z)
+    head = [(sum(HEAD[:i]), size, i) for i, size in enumerate(HEAD)]
     tail = [(BLOCK - CHUNK + sum(TAIL[:i]), size, REGULAR + i) for i, size in enumerate(TAIL)]
 
-    load_x, load_g, load_u, load_d = (
+    parts = [(src.at[layer, cols, :], dst.at[cols, :]) for cols in FFN_PARTS for src, dst in ((wg_ref, wg), (wu_ref, wu))]
+    load_x, load_g0, load_u0, load_g1, load_u1, load_d, load_rest = (
         pltpu.make_async_copy(src, dst, load_sem.at[i]) for i, (src, dst) in enumerate((
-            (x_ref, xv), (wg_ref.at[layer], wg), (wu_ref.at[layer], wu), (wd_ref.at[layer], wd))))
-    load_x.start()
-    load_g.start()
+            (x_ref.at[:CHUNK, :], xv.at[:CHUNK, :]), *parts,
+            (wd_ref.at[layer], wd), (x_ref.at[CHUNK:, :], xv.at[CHUNK:, :]))))
+    for load in (load_x, load_g0, load_u0):
+        load.start()
 
     signal(partner, cp)
     pl.when(inner)(lambda: signal(middle, cp))
@@ -710,7 +711,17 @@
         return rows_of(j, CHUNK)
 
     def piece(i):
-        return pl.multiple_of(i * PIECE, PIECE), PIECE, i
+        at = CHUNK + (i - len(head)) * PIECE
+        return pl.multiple_of(at, PIECE), PIECE, i
+
+    def pieces(j, action):
+        def run(parts):
+            for part in parts:
+                action(part)
+        pl.when(j == 0)(lambda: run(head))
+        pl.when((j > 0) & (j < CHUNKS - 1))(
+            lambda: run([piece(len(head) + (j - 1) * PER_CHUNK + k) for k in range(PER_CHUNK)]))
+        pl.when(j == CHUNKS - 1)(lambda: run(tail))
 
     def piece_copy(src, dst, send, recv, part, dev):
         at, size, i = part
@@ -729,23 +740,30 @@
         at, size, i = part
         return pltpu.make_async_copy(xv.at[pl.ds(at, size), :], out_ref.at[pl.ds(at, size), :], x_local.at[i])
 
+    def first(j, waits, *starts):
+        @pl.when(j == 0)
+        def _():
+            waits.wait()
+            for load in starts:
+                load.start()
+
     @scoped("activate")
-    def activate(j):
-        normed = normalize(xv[chunk_rows(j), :], gain)
-
-        @pl.when(j == 0)
-        def _():
-            load_g.wait()
-            load_u.start()
-            load_d.start()
-        gate = dot_rows(normed, wg[...])
-        pl.when(j == 0)(load_u.wait)
-        up = dot_rows(normed, wu[...])
-        act[...] = (gate * jax.nn.sigmoid(gate) * up).astype(BF16)
+    def activate(j, part):
+        cols = FFN_PARTS[part]
+        if part:
+            first(j, load_g1, load_d, load_rest)
+        else:
+            normed[...] = normalize(xv[chunk_rows(j), :], gain)
+            first(j, load_g0, load_g1, load_u1)
+        gate = dot_rows(normed[...], wg[cols, :])
+        first(j, load_u1 if part else load_u0)
+        up = dot_rows(normed[...], wu[cols, :])
+        act[:, cols] = (gate * jax.nn.sigmoid(gate) * up).astype(BF16)
 
     @scoped("down")
     def down(j):
         pl.when(j == 0)(load_d.wait)
+        pl.when(j == 0)(load_rest.wait)
         pv[chunk_rows(j), :] = jnp.dot(act[...], wd[...], preferred_element_type=F32).astype(BF16)
 
     @scoped("add_end")
@@ -785,31 +803,27 @@
 
         @scoped("x_wait")
         def x_wait(c):
-            def land(parts):
-                for part in parts:
-                    copy_x(part).wait_recv()
-                    copy_local(part).start()
-            pl.when(outer & (c < CHUNKS - 1))(lambda: land([piece(c * PER_CHUNK + k) for k in range(PER_CHUNK)]))
-            pl.when(outer & (c == CHUNKS - 1))(lambda: land(tail))
+            def land(part):
+                copy_x(part).wait_recv()
+                copy_local(part).start()
+            pl.when(outer)(lambda: pieces(c, land))
 
         def project(c):
             x_wait(c)
-            pl.when(c >= 1)(lambda: kv.near(c - 1))
 
             @pl.when(c >= 2)
             def _():
-                kv.diagonal(c - 2)
                 kv.own(c - 2, wait_send)
                 stores(c - 2, wait)
 
             with jax.named_scope("project"):
                 rows = chunk_rows(c)
                 slot = c % 2
-                normed = normalize(xv[rows, :], gain_n)
+                hidden = normalize(xv[rows, :], gain_n)
                 cos = cos_ref[rows, :]
                 sin = sin_ref[rows, :]
                 for which in range(3):
-                    proj = jnp.dot(normed, w_buf[which], preferred_element_type=F32)
+                    proj = jnp.dot(hidden, w_buf[which], preferred_element_type=F32)
                     for h in range(HEADS):
                         part = proj[:, h * HEAD_DIM:(h + 1) * HEAD_DIM] + bias_ref[h, which:which + 1, :].astype(F32)
                         if which < 2:
@@ -819,16 +833,29 @@
                             v_st[slot, h] = part.T.astype(BF16)
             kv.own(c)
             stores(c, start)
-
-    def serve(j, half):
-        @loop(0, PER_CHUNK // 2)
-        def _(k):
-            i = j * PER_CHUNK + half * (PER_CHUNK // 2) + k
+            pl.when(c >= 1)(lambda: kv.near(c - 1))
+            pl.when(c >= 2)(lambda: kv.diagonal(c - 2))
+
+    def serve(j, slot):
+        @pl.when(inner & (j == 1))
+        def _():
+            for i in HEAD_SLOTS[slot]:
+                add_end(head[i])
+                if i >= SKEW:
+                    add_middle(head[i - SKEW])
+
+        @pl.when(inner & (j > 1))
+        def _():
+            i = len(head) + (j - 2) * PER_CHUNK + slot
             add_end(piece(i))
-            pl.when(i >= SKEW)(lambda: add_middle(piece(i - SKEW)))
-
-    def serve_tail(first, last):
-        for i in range(first, last):
+            if slot < SKEW:
+                pl.when(j == 2)(lambda: add_middle(head[slot - SKEW]))
+                pl.when(j > 2)(lambda: add_middle(piece(i - SKEW)))
+            else:
+                add_middle(piece(i - SKEW))
+
+    def serve_tail(begin, last):
+        for i in range(begin, last):
             if i < len(tail):
                 add_end(tail[i])
             if i == 0:
@@ -842,19 +869,13 @@
 
     @loop(0, CHUNKS)
     def _(j):
-        activate(j)
-        pl.when(inner & (j >= 1))(lambda: serve(j - 1, 0))
+        activate(j, 0)
+        serve(j, 0)
+        activate(j, 1)
+        serve(j, 1)
         down(j)
-
-        @pl.when(outer & (j < CHUNKS - 1))
-        def _():
-            for k in range(PER_CHUNK):
-                copy_r(piece(j * PER_CHUNK + k)).start()
-
-        @pl.when(outer & (j == CHUNKS - 1))
-        def _():
-            for part in tail:
-                copy_r(part).start()
+        pl.when(outer)(lambda: pieces(j, lambda part: copy_r(part).start()))
+        serve(j, 2)
 
         if following:
             @pl.when(j == 0)
@@ -871,7 +892,7 @@
             pl.when(j == 5)(lambda: weights.diagonal(0))
             pl.when(j == 6)(lambda: weights.core(0))
             pl.when(j >= lag)(lambda: project(j - lag))
-        pl.when(inner & (j >= 1))(lambda: serve(j - 1, 1))
+        serve(j, 3)
 
     if following:
         @loop(CHUNKS - lag, CHUNKS)
@@ -911,17 +932,15 @@
             else:
                 copy_x(part).wait_recv()
 
-    @loop(0, REGULAR)
-    def _(i):
-        drain(piece(i))
-    for part in tail:
-        drain(part)
+    @loop(0, CHUNKS)
+    def _(j):
+        pieces(j, drain)
 
 
 def mlp_call(layer, *args):
     outs = [bf16(BLOCK, WIDTH)]
     in_specs = [hbm(), vmem(), hbm(), hbm(), hbm()]
-    scratch = [vmem_bf16(FFN, WIDTH)] * 3 + [vmem_bf16(BLOCK, WIDTH)] * 4 + [vmem_bf16(CHUNK, FFN), DMA((COLUMN,))]
+    scratch = [vmem_bf16(FFN, WIDTH)] * 3 + [vmem_bf16(BLOCK, WIDTH)] * 4 + [vmem_bf16(CHUNK, FFN), vmem_bf16(CHUNK, WIDTH), DMA((7,))]
     scratch += [DMA((REGULAR + len(TAIL),))] * 7
     aliases = {}
     if layer == 0:

time: 603 us -> 584 us (0.968)
  Pallas kernels: 586 us -> 567 us
    pallas_call x2, Pallas kernels: 324 us -> 311 us  [mlp_call(): pl.pallas_call(functools.partial(mlp_kernel, layer), out_shape=tuple(outs...]
where the time goes in v3:
time: 584 us
  Pallas kernels  567 us (97%)
  local copies, waits for them, and re-layouts  11.9 us (2%)
    pallas_call x2, Pallas kernels, mlp_call(): pl.pallas_call(functools.partial(mlp_kernel, layer), out_shape=tuple(outs...  311 us
    pallas_call x1, Pallas kernels, first_call(): pl.pallas_call(first_kernel, out_shape=(bf16(BLOCK, WIDTH), bf16(HEADS, B...  160 us
    pallas_call x1, Pallas kernels, second_call(): pl.pallas_call(second_kernel, out_shape=bf16(BLOCK, WIDTH), in_specs=[hbm...  95.3 us

profile of v3, /device:TPU:0, one launch (start us, length us, event | category | flops | bytes accessed | tf_op | source)
XLA Modules:
  0.0 584.0 jit_solution(6458407131892811927)
XLA Ops:
  0.6 0.7 convert_element_type.3
  1.3 0.8 slice_bitcast_fusion.2
  2.1 0.8 slice_bitcast_fusion.1
  2.9 0.8 slice_bitcast_fusion
  3.6 0.6 pad_maximum_fusion.2
  4.3 1.9 fusion
  6.2 1.3 pad_maximum_fusion
  7.5 160.4 %front0.1 = (bf16[1024,2560]{1,0:T(8,128)(2,1)}, bf16[5,1024,128]{2,1,0:T(8,128)(2,1)}, bf16[5,1024,128]{2,1,0:T(8,128)(2,1)}, bf16[5,3,8,16,2560]{4,3,2,1,0:T(8,128)(2,1)}, bf16[5,3,8,16,2560]{4,3,2,1,0:T(8,128)(2,1)}) custom-call(bf16[1024,2560]{1,0:T(8,128)(2,1)} %x_ref.1, bf16[2,2560]{1,0:T(2,128)(2,1)} %refs_5_.1, bf16[2,2560,640]{2,1,0:T(8,128)(2,1)} %refs_6_.1, ...), custom_call_target="tpu_custom_call" | custom-call | flops 70000001024 | bytes 50000000 | tf_op jit(solution)/shard_map/front0/pallas_call | solution.py:571
  167.9 169.4 %mlp0.1 = (bf16[1024,2560]{1,0:T(8,128)(2,1)}, bf16[5,1024,128]{2,1,0:T(8,128)(2,1)}, bf16[5,1024,128]{2,1,0:T(8,128)(2,1)}, bf16[5,1024,128]{2,1,0:T(8,128)(2,1...) custom-call(bf16[1024,2560]{1,0:T(8,128)(2,1)} %get-tuple-element.16, ...), custom_call_target="tpu_custom_call", output_to_operand_aliasing={{6}: (12, {})} | custom-call | flops 99999997952 | bytes 50000000 | tf_op jit(solution)/shard_map/mlp0/pallas_call | solution.py:953
  337.3 95.3 %front1.1.refs_0_ = bf16[1024,2560]{1,0:T(8,128)(2,1)} custom-call(bf16[1024,2560]{1,0:T(8,128)(2,1)} %get-tuple-element.18.x_ref, bf16[5,1024,128]{2,1,0:T(8,128)(2,1)} %get-tuple-element.19.q_ref, bf16[5,8,1024,128]{3,2,1,0:T(8,128)(2,1)} %get-tuple-element.20.k_ref, bf16[5,8,128,1024]{3,2,1,0:T(8,128)(2,1)} %get-tuple-element.21.v_ref, ...), custom_call_target="tpu_custom_call" | custom-call | flops 49999998976 | bytes 50000000 | tf_op jit(solution)/shard_map/front1/pallas_call | solution.py:650
  432.6 141.8 %mlp1.1 = bf16[1024,2560]{1,0:T(8,128)(2,1)} custom-call(bf16[1024,2560]{1,0:T(8,128)(2,1)} %front1.1.refs_0_, bf16[2,2560]{1,0:T(2,128)(2,1)} %refs_1_.3, bf16[2,1728,2560]{2,1,0:T(8,128)(2,1)} %bitcast.24, bf16[2,1728,2560]{2,1,0:T(8,128)(2,1)} %bitcast.26, bf16[2,1728,2560]{2,1,0:T(8,128)(2,1)} %refs_4_.3), custom_call_target="tpu_custom_call" | custom-call | flops 99999997952 | bytes 50000000 | tf_op jit(solution)/shard_map/mlp1/pallas_call | solution.py:953
  574.3 0.0 copy-start.1
  574.3 0.0 copy-start
  574.4 0.0 copy-start.3
  574.4 5.4 copy.26
  579.7 0.0 copy-done.1
  579.7 0.0 copy-start.2
  579.7 1.1 copy.27
  580.8 0.0 copy-done
  580.8 1.1 copy.28
  581.8 0.0 copy-done.3
  581.8 1.1 copy.29
  582.9 0.0 copy-done.2
  582.9 1.1 copy.30
  (1 shorter events, 0.0 us)
Async XLA Ops:
  574.3 5.4 copy-start.1
  574.3 6.4 %copy-start = (bf16[5,1024,128]{2,1,0:T(8,128)(2,1)S(1)}, bf16[5,1024,128]{2,1,0:T(8,128)(2,1)}, u32[]{:S(2)}) copy-start(bf16[5,1024,128]{2,1,0:T(8,128)(2,1)} %get-tuple-element.24) | copy-start | bytes 3932164
  574.4 7.5 %copy-start.3 = (bf16[5,1024,128]{2,1,0:T(8,128)(2,1)S(1)}, bf16[5,1024,128]{2,1,0:T(8,128)(2,1)}, u32[]{:S(2)}) copy-start(bf16[5,1024,128]{2,1,0:T(8,128)(2,1)} %get-tuple-element.25) | copy-start | bytes 3932164
  579.7 3.2 copy-start.2

commit v4 on v3

--- a/solution.py
+++ b/solution.py
@@ -437,7 +437,7 @@
         load_wo=load_wo, apply_wo=apply_wo, drain=drain, settle=settle)
 
 
-def first_kernel(x_ref, gain_ref, wq_ref, wk_ref, wv_ref, bias_ref, cos_ref, sin_ref, wo_ref,
+def first_kernel(x_ref, gain_ref, wq_ref, wk_ref, wv_ref, bq_ref, bk_ref, bv_ref, cos_ref, sin_ref, wo_ref,
                  out_ref, k_out, v_out, full_ref, next_ref,
                  w_buf, k_buf, v_buf, v_nat, w_sem, kv_sem, send_sem, recv_sem, *rest):
     z = lax.axis_index("tp")
@@ -486,7 +486,8 @@
         def _(i):
             rows = rows_of(i, TILE_Q)
             proj = jnp.dot(xh[rows, :], w_buf[h % 2], preferred_element_type=F32)
-            q, k, v = (proj[:, n * HEAD_DIM:(n + 1) * HEAD_DIM] + bias_ref[h, n:n + 1, :].astype(F32) for n in range(3))
+            q, k, v = (proj[:, n * HEAD_DIM:(n + 1) * HEAD_DIM] + bias[:1, lanes_of(h)].astype(F32)
+                       for n, bias in enumerate((bq_ref, bk_ref, bv_ref)))
             cos = cos_ref[rows, :]
             sin = sin_ref[rows, :]
             q_buf[h, rows, :] = rotate(q, cos, sin)
@@ -541,6 +542,14 @@
 
     weights.near(1)
     weights.own(3)
+
+    @loop(0, HEADS)
+    def _(h):
+        kv.drain(h)
+        caches(h, wait)
+    next_slices.finish()
+    next_slices.drain()
+    slices.drain()
     weights.diagonal(0)
 
     @loop(0, HEADS)
@@ -556,14 +565,8 @@
 
     @loop(0, HEADS)
     def _(h):
-        kv.drain(h)
         weights.drain(h)
-        caches(h, wait)
         parts.drain(h)
-
-    next_slices.finish()
-    next_slices.drain()
-    slices.drain()
     parts.settle()
 
 
@@ -572,7 +575,7 @@
         first_kernel,
         out_shape=(bf16(BLOCK, WIDTH), bf16(HEADS, BLOCK, HEAD_DIM), bf16(HEADS, BLOCK, HEAD_DIM),
                    bf16(*FULL_SHAPE), bf16(*FULL_SHAPE)),
-        in_specs=[hbm(), vmem(), hbm(), hbm(), hbm(), vmem(), vmem(), vmem(), hbm()],
+        in_specs=[hbm(), vmem(), hbm(), hbm(), hbm()] + [vmem()] * 5 + [hbm()],
         out_specs=(hbm(),) * 5,
         scratch_shapes=[
             vmem_bf16(2, WIDTH, 3 * HEAD_DIM),
@@ -673,7 +676,7 @@
     following = layer == 0
     x_ref, gain_ref, wg_ref, wu_ref, wd_ref, *refs = refs
     if following:
-        next_gain, wq_ref, wk_ref, wv_ref, bias_ref, cos_ref, sin_ref, _, *refs = refs
+        next_gain, wq_ref, wk_ref, wv_ref, bq_ref, bk_ref, bv_ref, cos_ref, sin_ref, _, *refs = refs
         out_ref, q_out, k_out, v_out, k_all, v_all, full_ref, *refs = refs
     else:
         out_ref, *refs = refs
@@ -822,10 +825,11 @@
                 hidden = normalize(xv[rows, :], gain_n)
                 cos = cos_ref[rows, :]
                 sin = sin_ref[rows, :]
-                for which in range(3):
+                for which, bias in enumerate((bq_ref, bk_ref, bv_ref)):
                     proj = jnp.dot(hidden, w_buf[which], preferred_element_type=F32)
+                    proj += bias[layer + 1:layer + 2, :].astype(F32)
                     for h in range(HEADS):
-                        part = proj[:, h * HEAD_DIM:(h + 1) * HEAD_DIM] + bias_ref[h, which:which + 1, :].astype(F32)
+                        part = proj[:, h * HEAD_DIM:(h + 1) * HEAD_DIM]
                         if which < 2:
                             (q_st, k_st)[which][slot, h] = rotate(part, cos, sin)
                         else:
@@ -864,6 +868,26 @@
             elif i >= TAIL_SKEW:
                 add_middle(tail[i - TAIL_SKEW])
 
+    def drain(part):
+        @pl.when(inner)
+        def _():
+            copy_s(part).wait_send()
+            copy_x(part).wait_send()
+            copy_local(part).wait()
+
+        @pl.when(outer)
+        def _():
+            copy_r(part).wait_send()
+            if following:
+                copy_local(part).wait()
+            else:
+                copy_x(part).wait_recv()
+
+    def drain_pieces():
+        @loop(0, CHUNKS)
+        def _(j):
+            pieces(j, drain)
+
     tail_end = len(tail) + TAIL_SKEW
     lag = jnp.where(inner, 2, 5)
 
@@ -900,41 +924,26 @@
             pl.when(inner & (c == CHUNKS - 2))(lambda: serve_tail(0, 1))
             pl.when(inner & (c == CHUNKS - 1))(lambda: serve_tail(1, tail_end))
             project(c)
+
+        def settle(lo, hi):
+            @loop(lo, hi)
+            def _(c):
+                kv.core(c)
+                kv.drain(c, False)
+
+        settle(0, CHUNKS - 2)
+        weights.drain(0)
+        drain_pieces()
         kv.near(CHUNKS - 1)
         kv.diagonal(CHUNKS - 2)
         kv.diagonal(CHUNKS - 1)
-
-        @loop(0, CHUNKS)
-        def _(c):
-            kv.core(c)
-            kv.drain(c, False)
-
-            @pl.when(c >= CHUNKS - 2)
-            def _():
-                kv.own(c, wait_send)
-                stores(c, wait)
-        weights.drain(0)
+        for c in (CHUNKS - 2, CHUNKS - 1):
+            kv.own(c, wait_send)
+            stores(c, wait)
+        settle(CHUNKS - 2, CHUNKS)
     else:
         pl.when(inner)(lambda: serve_tail(0, tail_end))
-
-    def drain(part):
-        @pl.when(inner)
-        def _():
-            copy_s(part).wait_send()
-            copy_x(part).wait_send()
-            copy_local(part).wait()
-
-        @pl.when(outer)
-        def _():
-            copy_r(part).wait_send()
-            if following:
-                copy_local(part).wait()
-            else:
-                copy_x(part).wait_recv()
-
-    @loop(0, CHUNKS)
-    def _(j):
-        pieces(j, drain)
+        drain_pieces()
 
 
 def mlp_call(layer, *args):
@@ -946,7 +955,7 @@
     if layer == 0:
         outs += [bf16(HEADS, BLOCK, HEAD_DIM)] * 3
         outs += [bf16(HEADS, BLOCKS, BLOCK, HEAD_DIM), bf16(HEADS, BLOCKS, HEAD_DIM, BLOCK), bf16(*FULL_SHAPE)]
-        in_specs += [vmem(), hbm(), hbm(), hbm(), vmem(), vmem(), vmem(), hbm()]
+        in_specs += [vmem(), hbm(), hbm(), hbm()] + [vmem()] * 5 + [hbm()]
         aliases = {len(in_specs) - 1: len(outs) - 1}
         scratch += [vmem_bf16(3, WIDTH, HEADS * HEAD_DIM)] + [vmem_bf16(2, HEADS, CHUNK, HEAD_DIM)] * 4
         scratch += [DMA((3,)), DMA((2, 5))] + plane_sems(CHUNKS) + plane_sems(1)
@@ -963,6 +972,33 @@
     )(*args)
 
 
+def finish_kernel(*refs):
+    sources, results, (x_buf, c_buf, in_sem, out_sem) = refs[:5], refs[5:10], refs[10:]
+    steps = [(sources[0].at[rows_of(i), :], x_buf.at[rows_of(i), :], results[0].at[rows_of(i), :]) for i in range(BLOCK // ROWS)]
+    steps += [(src, c_buf.at[i], dst) for i, (src, dst) in enumerate(zip(sources[1:], results[1:]))]
+    loads = [pltpu.make_async_copy(src, buf, in_sem.at[i]) for i, (src, buf, _) in enumerate(steps)]
+    stores = [pltpu.make_async_copy(buf, dst, out_sem.at[i]) for i, (_, buf, dst) in enumerate(steps)]
+    for load in loads:
+        load.start()
+    for load, store in zip(loads, stores):
+        load.wait()
+        store.start()
+    for store in stores:
+        store.wait()
+
+
+def finish_call(*args):
+    return pl.pallas_call(
+        finish_kernel,
+        out_shape=tuple(bf16(*arg.shape) for arg in args),
+        in_specs=[hbm()] * len(args),
+        out_specs=(hbm(),) * len(args),
+        scratch_shapes=[vmem_bf16(BLOCK, WIDTH), vmem_bf16(4, HEADS, BLOCK, HEAD_DIM), DMA((8,)), DMA((8,))],
+        compiler_params=pltpu.CompilerParams(vmem_limit_bytes=VMEM_LIMIT),
+        name="finish",
+    )(*args)
+
+
 def solution(mesh):
     def local_step(x_in, positions, attn_gain, mlp_gain, w_query, b_query, w_key, b_key, w_value, b_value,
                    w_out, w_gate, w_up, w_down):
@@ -975,14 +1011,14 @@
         w_gate = jnp.swapaxes(w_gate, 1, 2)
         w_up = jnp.swapaxes(w_up, 1, 2)
         wo = w_out.reshape(2, HEADS, BLOCKS, SLICE, WIDTH)
-        bias = [jnp.stack([b.reshape(2, HEADS, HEAD_DIM)[layer] for b in (b_query, b_key, b_value)], axis=1)
-                for layer in range(2)]
-        hidden, k0, v0, _, full1 = first_call(x_in, attn_gain, w_query, w_key, w_value, bias[0], cos, sin, wo)
+        biases = (b_query, b_key, b_value)
+        hidden, k0, v0, _, full1 = first_call(x_in, attn_gain, w_query, w_key, w_value, *biases, cos, sin, wo)
         hidden, q, k1, v1, k_all, v_all, full1 = mlp_call(
-            0, hidden, mlp_gain, w_gate, w_up, w_down, attn_gain, w_query, w_key, w_value, bias[1], cos, sin, full1)
+            0, hidden, mlp_gain, w_gate, w_up, w_down, attn_gain, w_query, w_key, w_value, *biases, cos, sin, full1)
         hidden = second_call(hidden, q, k_all, v_all, wo, full1)
         hidden, = mlp_call(1, hidden, mlp_gain, w_gate, w_up, w_down)
-        return (hidden,) + tuple(jnp.swapaxes(cache, 0, 1) for cache in (k0, v0, k1, v1))
+        hidden, *caches = finish_call(hidden, k0, v0, k1, v1)
+        return (hidden,) + tuple(jnp.swapaxes(cache, 0, 1) for cache in caches)
 
     weight_col = P(None, None, "tp")
     bias_col = P(None, "tp")

time: 584 us -> 579 us (level)
  local copies, waits for them, and re-layouts: 11.9 us -> 0 us
  Pallas kernels: 567 us -> 574 us
    unnamed x13 -> x0, local copies, waits for them, and re-layouts: 9.59 us -> none
    pallas_call x0 -> x1, Pallas kernels: none -> 8.1 us  [finish_call(): pl.pallas_call(finish_kernel, out_shape=tuple((bf16(*arg.shape) for arg i...]
where the time goes in v4:
time: 579 us; the launch traced here: 578 us
  Pallas kernels  574 us (99%)
    pallas_call x2, Pallas kernels, mlp_call(): pl.pallas_call(functools.partial(mlp_kernel, layer), out_shape=tuple(outs...  310 us
    pallas_call x1, Pallas kernels, first_call(): pl.pallas_call(first_kernel, out_shape=(bf16(BLOCK, WIDTH), bf16(HEADS, B...  160 us
    pallas_call x1, Pallas kernels, second_call(): pl.pallas_call(second_kernel, out_shape=bf16(BLOCK, WIDTH), in_specs=[hbm...  95.3 us

profile of v4, /device:TPU:0, one launch (start us, length us, event | category | flops | bytes accessed | tf_op | source)
XLA Modules:
  0.0 578.3 jit_solution(7315171028386976849)
XLA Ops:
  0.6 0.7 convert_element_type.3
  1.3 1.9 fusion
  3.2 1.3 pad_maximum_fusion
  4.6 160.5 %front0.1 = (bf16[1024,2560]{1,0:T(8,128)(2,1)}, bf16[5,1024,128]{2,1,0:T(8,128)(2,1)}, bf16[5,1024,128]{2,1,0:T(8,128)(2,1)}, bf16[5,3,8,16,2560]{4,3,2,1,0:T(8,128)(2,1)}, bf16[5,3,8,16,2560]{4,3,2,1,0:T(8,128)(2,1)}) custom-call(bf16[1024,2560]{1,0:T(8,128)(2,1)} %x_ref.1, bf16[2,2560]{1,0:T(2,128)(2,1)} %refs_5_.1, bf16[2,2560,640]{2,1,0:T(8,128)(2,1)} %refs_6_.1, ...), custom_call_target="tpu_custom_call" | custom-call | flops 70000001024 | bytes 50000000 | tf_op jit(solution)/shard_map/front0/pallas_call | solution.py:574
  165.0 167.9 %mlp0.1 = (bf16[1024,2560]{1,0:T(8,128)(2,1)}, bf16[5,1024,128]{2,1,0:T(8,128)(2,1)}, bf16[5,1024,128]{2,1,0:T(8,128)(2,1)}, bf16[5,1024,128]{2,1,0:T(8,128)(2,1...) custom-call(bf16[1024,2560]{1,0:T(8,128)(2,1)} %get-tuple-element.21, ...), custom_call_target="tpu_custom_call", output_to_operand_aliasing={{6}: (14, {})} | custom-call | flops 99999997952 | bytes 50000000 | tf_op jit(solution)/shard_map/mlp0/pallas_call | solution.py:962
  332.9 95.3 %front1.1.refs_0_ = bf16[1024,2560]{1,0:T(8,128)(2,1)} custom-call(bf16[1024,2560]{1,0:T(8,128)(2,1)} %get-tuple-element.23.x_ref, bf16[5,1024,128]{2,1,0:T(8,128)(2,1)} %get-tuple-element.24.q_ref, bf16[5,8,1024,128]{3,2,1,0:T(8,128)(2,1)} %get-tuple-element.25.k_ref, bf16[5,8,128,1024]{3,2,1,0:T(8,128)(2,1)} %get-tuple-element.26.v_ref, ...), custom_call_target="tpu_custom_call" | custom-call | flops 49999998976 | bytes 50000000 | tf_op jit(solution)/shard_map/front1/pallas_call | solution.py:653
  428.2 141.8 %mlp1.1.refs_0_ = bf16[1024,2560]{1,0:T(8,128)(2,1)} custom-call(bf16[1024,2560]{1,0:T(8,128)(2,1)} %front1.1.refs_0_, bf16[2,2560]{1,0:T(2,128)(2,1)} %refs_1_.3, bf16[2,1728,2560]{2,1,0:T(8,128)(2,1)} %bitcast.8, bf16[2,1728,2560]{2,1,0:T(8,128)(2,1)} %bitcast.10, bf16[2,1728,2560]{2,1,0:T(8,128)(2,1)} %refs_4_.3), custom_call_target="tpu_custom_call" | custom-call | flops 99999997952 | bytes 50000000 | tf_op jit(solution)/shard_map/mlp1/pallas_call | solution.py:962
  570.0 8.1 %finish.1 = (bf16[1024,2560]{1,0:T(8,128)(2,1)}, bf16[5,1024,128]{2,1,0:T(8,128)(2,1)}, bf16[5,1024,128]{2,1,0:T(8,128)(2,1)}, bf16[5,1024,128]{2,1,0:T(8,128)(2,1)}, bf16[5,1024,128]{2,1,0:T(8,128)(2,1)}) custom-call(bf16[1024,2560]{1,0:T(8,128)(2,1)} %mlp1.1.refs_0_, bf16[5,1024,128]{2,1,0:T(8,128)(2,1)} %get-tuple-element.28.refs_1_, ...), custom_call_target="tpu_custom_call" | custom-call | tf_op jit(solution)/shard_map/finish/pallas_call | solution.py:991
  (1 shorter events, 0.0 us)
